TPU v7x, 1024 devices: a whole 4x8x16 slice. The times are simulated.
1024 devices in a mesh: gx: 4 (over x), gy: 16 (over y, core), gz: 16 (over z).
Axes of the slice: x: 4, y: 8, z: 16, core: 2. Of those that a mesh axis runs over, the one named last changes fastest.
Arguments:
- right_side: float32 [48, 256, 2048], P('gx', 'gy', 'gz'), may hold values from -8 to 8
- coefficient: float32 [48, 256, 2048], P('gx', 'gy', 'gz'), may hold values from 0.02 to 1
Outputs:
- solution: float32 [48, 256, 2048], P('gx', 'gy', 'gz')
- residual: float32 [48, 256, 2048], P('gx', 'gy', 'gz')
- precond: float32 [48, 256, 2048], P('gx', 'gy', 'gz')
- image: float32 [48, 256, 2048], P('gx', 'gy', 'gz')
All inputs are finite; a program needn't handle non-finite values.
Results may differ from a plain program's by a relative error of at most 0.00021.
Values sent between devices are 32-bit elements; how exact they have to be, the bound alone decides.
A program may use at most 32 MiB of HBM per device.

v0:
```python
import jax
import jax.numpy as jnp
from jax import lax
from jax.sharding import Mesh
from jax.sharding import PartitionSpec as P

SWEEPS = 4
GX_GY_GZ = ("gx", "gy_0", "gy_1", "gz")
GY = ("gy_0", "gy_1")


relaxation = 0.6


def with_halo(block, sides, width):
    for axis, dim in sides:
        count = lax.axis_size(axis)
        forward = [(i, i + 1) for i in range(count - 1)]
        backward = [(target, source) for source, target in forward]
        low = lax.ppermute(
            lax.slice_in_dim(block, block.shape[dim] - width, None, axis=dim), axis, forward
        )
        high = lax.ppermute(lax.slice_in_dim(block, 0, width, axis=dim), axis, backward)
        block = jnp.concatenate([low, block, high], axis=dim)
    return block


def over_axes(array, axes):
    for axis in axes:
        array = lax.psum(array, axis)
    return array


def block_sum(padded):
    summed = padded[:-2] + padded[1:-1] + padded[2:]
    summed = summed[:, :-2] + summed[:, 1:-1] + summed[:, 2:]
    return summed[:, :, :-2] + summed[:, :, 1:-1] + summed[:, :, 2:]


def restrict(values):
    extent = values.shape
    grouped = values.reshape(extent[0] // 2, 2, extent[1] // 2, 2, extent[2] // 2, 2)
    return 0.5 * grouped.sum(axis=(1, 3, 5))


def prolong(values):
    return jnp.repeat(jnp.repeat(jnp.repeat(values, 2, axis=0), 2, axis=1), 2, axis=2)


def stencil(values, reaction):
    padded = with_halo(values, (("gx", 0), (GY, 1), ("gz", 2)), 1)
    return (27.0 + reaction) * values - block_sum(padded)


def spread_deep(source, reaction):
    margin = SWEEPS - 1
    stacked = jnp.stack([source, reaction, jnp.ones_like(source)])
    widened = with_halo(stacked, (("gx", 1), (GY, 2), ("gz", 3)), margin)
    wide_source = widened[0]
    wide_reaction = widened[1]
    inside = widened[2]
    correction = relaxation * wide_source / (26.0 + wide_reaction)
    for sweep in range(SWEEPS - 1):
        applied = (27.0 + wide_reaction) * correction - block_sum(jnp.pad(correction, 1))
        correction = (
            correction + relaxation * (wide_source - applied) / (26.0 + wide_reaction)
        ) * inside
    return correction[margin:-margin, margin:-margin, margin:-margin]


def coarsest(source, reaction):
    return spread_deep(source, reaction)


def multigrid(source, reactions, level_index):
    if level_index == 2:
        return coarsest(source, reactions[2])
    reaction = reactions[level_index]
    correction = relaxation * source / (26.0 + reaction)
    remainder = source - stencil(correction, reaction)
    correction = correction + prolong(multigrid(restrict(remainder), reactions, level_index + 1))
    return correction + relaxation * (source - stencil(correction, reaction)) / (26.0 + reaction)


def shards(right_side, coefficient):
    middle = restrict(coefficient)
    reactions = (coefficient, middle, restrict(middle))
    residual = right_side
    precond = multigrid(residual, reactions, 0)
    image = stencil(precond, coefficient)
    gamma_now = over_axes(jnp.sum(residual * precond), GX_GY_GZ)
    delta_now = over_axes(jnp.sum(image * precond), GX_GY_GZ)
    precond_image = multigrid(image, reactions, 0)
    image_twice = stencil(precond_image, coefficient)
    alpha_now = gamma_now / delta_now
    direction = precond
    dir_image = image
    solution = alpha_now * direction
    residual = residual - alpha_now * dir_image
    precond = precond - alpha_now * precond_image
    image = image - alpha_now * image_twice
    return (solution, residual, precond, image)


def solution(mesh):
    torus = Mesh(
        mesh.devices.reshape(mesh.shape["gx"], 8, 2, mesh.shape["gz"]), ("gx", "gy_0", "gy_1", "gz")
    )
    return jax.shard_map(
        shards,
        mesh=torus,
        in_specs=(P("gx", GY, "gz"), P("gx", GY, "gz")),
        out_specs=(P("gx", GY, "gz"), P("gx", GY, "gz"), P("gx", GY, "gz"), P("gx", GY, "gz")),
        check_vma=False,
    )
```

profile of v0, /device:TPU:1, one launch (start us, length us, event | category | flops | bytes accessed | tf_op | source)
XLA Modules:
  0.0 435.0 jit_solution(11102172605339193236)
XLA Ops:
  1.6 3.9 collective-permute-start
  6.9 3.1 collective-permute-done.1
  10.0 5.2 %collective-permute-start.2 = (f32[14,1,128]{2,1,0:T(1,128)S(1)}, f32[14,1,128]{2,1,0:T(1,128)S(1)}, u32[]{:S(2)}, u32[]{:S(2)}) collective-permute-start(f32[14,1,128]{2,1,0:T(1,128)S(1)} %get-tuple-element.89), channel_id=1, source_target_pairs={{0,16},{16,32},{32,48},{48,64},{64,80},{80,96},{96,112},{112,128},... | collective-permute-start | bytes 21512 | tf_op jit(solution)/shard_map/ppermute | solution.py:20
  15.2 10.6 %collective-permute-start.3 = (f32[14,1,128]{2,1,0:T(1,128)S(1)}, f32[14,1,128]{2,1,0:T(1,128)S(1)}, u32[]{:S(2)}, u32[]{:S(2)}) collective-permute-start(f32[14,1,128]{2,1,0:T(1,128)S(1)} %get-tuple-element.88), channel_id=1, source_target_pairs={{16,0},{32,16},{48,32},{64,48},{80,64},{96,80},{112,96},{128,112},... | collective-permute-start | bytes 21512 | tf_op jit(solution)/shard_map/ppermute | solution.py:23
  29.3 8.4 %reshape.99 = f32[6,2,8,2,64,2]{5,4,3,2,1,0:T(8,128)} reshape(f32[12,16,128]{2,1,0:T(8,128)} %param.3) | data formatting | bytes 196608 | tf_op jit(solution)/shard_map/reshape | solution.py:42
  37.7 3.3 reduce_sum.73
  41.9 7.6 %reshape.98 = f32[6,2,8,2,64,2]{5,4,3,2,1,0:T(8,128)} reshape(f32[12,16,128]{2,1,0:T(8,128)S(1)} %fusion.37) | data formatting | bytes 196608 | tf_op jit(solution)/shard_map/reshape | solution.py:42
  49.5 3.3 reduce_sum.72
  55.5 3.0 collective-permute-done.7
  60.5 3.1 collective-permute-start.9
  65.5 4.3 collective-permute-start.10
  71.1 4.1 collective-permute-done.11
  78.7 4.0 collective-permute-start.12
  83.6 4.2 collective-permute-start.14
  89.8 3.5 collective-permute-done.15
  93.5 5.2 %collective-permute-start.16 = (f32[3,9,10,3]{3,2,1,0:T(8,128)S(1)}, f32[3,9,10,3]{3,2,1,0:T(8,128)S(1)}, u32[]{:S(2)}, u32[]{:S(2)}) collective-permute-start(f32[3,9,10,3]{3,2,1,0:T(8,128)S(1)} %get-tuple-element.64), channel_id=1, source_target_pairs={{0,1},{1,2},{2,3},{3,4},{4,5},{5,6},{6,7},{7,8},{8,9},{9,10},{10,1... | collective-permute-start | bytes 9728 | tf_op jit(solution)/shard_map/ppermute | solution.py:20
  102.1 5.3 %collective-permute-done.17 = f32[3,9,10,3]{3,2,1,0:T(8,128)S(1)} collective-permute-done((f32[3,9,10,3]{3,2,1,0:T(8,128)S(1)}, f32[3,9,10,3]{3,2,1,0:T(8,128)S(1)}, u32[]{:S(2)}, u32[]{:S(2)}) %collective-permute-start.17) | collective-permute-done | bytes 3272 | tf_op jit(solution)/shard_map/ppermute | solution.py:23
  109.0 3.9 collective-permute-start.18
  114.2 3.0 collective-permute-done.19
  117.3 5.6 %collective-permute-start.20 = (f32[8,1,64]{2,1,0:T(1,128)S(1)}, f32[8,1,64]{2,1,0:T(1,128)S(1)}, u32[]{:S(2)}, u32[]{:S(2)}) collective-permute-start(f32[8,1,64]{2,1,0:T(1,128)S(1)} %get-tuple-element.134), channel_id=1, source_target_pairs={{0,16},{16,32},{32,48},{48,64},{64,80},{80,96},{96,112},{112,128},... | collective-permute-start | bytes 6152 | tf_op jit(solution)/shard_map/ppermute | solution.py:20
  124.8 3.0 collective-permute-done.21
  127.9 4.9 %collective-permute-start.22 = (f32[8,10,1]{2,0,1:T(8,128)S(1)}, f32[8,10,1]{2,0,1:T(8,128)S(1)}, u32[]{:S(2)}, u32[]{:S(2)}) collective-permute-start(f32[8,10,1]{2,0,1:T(8,128)S(1)} %get-tuple-element.123), channel_id=1, source_target_pairs={{0,1},{1,2},{2,3},{3,4},{4,5},{5,6},{6,7},{7,8},{8,9},{9,10},{10,1... | collective-permute-start | bytes 968 | tf_op jit(solution)/shard_map/ppermute | solution.py:20
  134.1 4.0 collective-permute-done.23
  143.3 3.4 collective-permute-done.25
  146.8 4.6 %collective-permute-start.26 = (f32[14,1,128]{2,1,0:T(1,128)S(1)}, f32[14,1,128]{2,1,0:T(1,128)S(1)}, u32[]{:S(2)}, u32[]{:S(2)}) collective-permute-start(f32[14,1,128]{2,1,0:T(1,128)S(1)} %get-tuple-element.87), channel_id=1, source_target_pairs={{0,16},{16,32},{32,48},{48,64},{64,80},{80,96},{96,112},{112,128},... | collective-permute-start | bytes 21512 | tf_op jit(solution)/shard_map/ppermute | solution.py:20
  153.3 3.0 collective-permute-done.27
  156.4 3.7 collective-permute-start.28
  162.3 5.0 %collective-permute-done.29 = f32[14,18,1]{2,0,1:T(8,128)S(1)} collective-permute-done((f32[14,18,1]{2,0,1:T(8,128)S(1)}, f32[14,18,1]{2,0,1:T(8,128)S(1)}, u32[]{:S(2)}, u32[]{:S(2)}) %collective-permute-start.29) | collective-permute-done | bytes 1040 | tf_op jit(solution)/shard_map/ppermute | solution.py:23
  171.2 3.5 collective-permute-done.31
  174.7 5.0 %collective-permute-start.32 = (f32[14,1,128]{2,1,0:T(1,128)S(1)}, f32[14,1,128]{2,1,0:T(1,128)S(1)}, u32[]{:S(2)}, u32[]{:S(2)}) collective-permute-start(f32[14,1,128]{2,1,0:T(1,128)S(1)} %get-tuple-element.85), channel_id=1, source_target_pairs={{0,16},{16,32},{32,48},{48,64},{64,80},{80,96},{96,112},{112,128},... | collective-permute-start | bytes 21512 | tf_op jit(solution)/shard_map/ppermute | solution.py:20
  184.7 5.2 %collective-permute-start.34 = (f32[14,18,1]{2,0,1:T(8,128)S(1)}, f32[14,18,1]{2,0,1:T(8,128)S(1)}, u32[]{:S(2)}, u32[]{:S(2)}) collective-permute-start(f32[14,18,1]{2,0,1:T(8,128)S(1)} %get-tuple-element.72), channel_id=1, source_target_pairs={{0,1},{1,2},{2,3},{3,4},{4,5},{5,6},{6,7},{7,8},{8,9},{9,10},{10,1... | collective-permute-start | bytes 3032 | tf_op jit(solution)/shard_map/ppermute | solution.py:20
  192.1 4.7 %collective-permute-done.35 = f32[14,18,1]{2,0,1:T(8,128)S(1)} collective-permute-done((f32[14,18,1]{2,0,1:T(8,128)S(1)}, f32[14,18,1]{2,0,1:T(8,128)S(1)}, u32[]{:S(2)}, u32[]{:S(2)}) %collective-permute-start.35) | collective-permute-done | bytes 1040 | tf_op jit(solution)/shard_map/ppermute | solution.py:23
  200.8 3.5 collective-permute-done.37
  204.3 5.1 %collective-permute-start.38 = (f32[14,1,128]{2,1,0:T(1,128)S(1)}, f32[14,1,128]{2,1,0:T(1,128)S(1)}, u32[]{:S(2)}, u32[]{:S(2)}) collective-permute-start(f32[14,1,128]{2,1,0:T(1,128)S(1)} %get-tuple-element.83), channel_id=1, source_target_pairs={{0,16},{16,32},{32,48},{48,64},{64,80},{80,96},{96,112},{112,128},... | collective-permute-start | bytes 21512 | tf_op jit(solution)/shard_map/ppermute | solution.py:20
  214.5 4.5 %collective-permute-start.40 = (f32[14,18,1]{2,0,1:T(8,128)S(1)}, f32[14,18,1]{2,0,1:T(8,128)S(1)}, u32[]{:S(2)}, u32[]{:S(2)}) collective-permute-start(f32[14,18,1]{2,0,1:T(8,128)S(1)} %get-tuple-element.70), channel_id=1, source_target_pairs={{0,1},{1,2},{2,3},{3,4},{4,5},{5,6},{6,7},{7,8},{8,9},{9,10},{10,1... | collective-permute-start | bytes 3032 | tf_op jit(solution)/shard_map/ppermute | solution.py:20
  221.2 4.4 %collective-permute-done.41 = f32[14,18,1]{2,0,1:T(8,128)S(1)} collective-permute-done((f32[14,18,1]{2,0,1:T(8,128)S(1)}, f32[14,18,1]{2,0,1:T(8,128)S(1)}, u32[]{:S(2)}, u32[]{:S(2)}) %collective-permute-start.41) | collective-permute-done | bytes 1040 | tf_op jit(solution)/shard_map/ppermute | solution.py:23
  226.4 7.6 %reshape.107 = f32[6,2,8,2,64,2]{5,4,3,2,1,0:T(8,128)} reshape(f32[12,16,128]{2,1,0:T(8,128)S(1)} %fusion.29) | data formatting | bytes 196608 | tf_op jit(solution)/shard_map/reshape | solution.py:42
  234.0 3.3 reduce_sum.78
  240.3 3.4 collective-permute-done.43
  243.7 4.7 %collective-permute-start.44 = (f32[8,1,64]{2,1,0:T(1,128)S(1)}, f32[8,1,64]{2,1,0:T(1,128)S(1)}, u32[]{:S(2)}, u32[]{:S(2)}) collective-permute-start(f32[8,1,64]{2,1,0:T(1,128)S(1)} %get-tuple-element.132), channel_id=1, source_target_pairs={{0,16},{16,32},{32,48},{48,64},{64,80},{80,96},{96,112},{112,128},... | collective-permute-start | bytes 6152 | tf_op jit(solution)/shard_map/ppermute | solution.py:20
  250.3 3.0 collective-permute-done.45
  253.3 3.6 collective-permute-start.46
  258.3 3.8 collective-permute-done.47
  264.6 4.0 collective-permute-start.48
  269.5 4.2 collective-permute-start.50
  275.7 3.5 collective-permute-done.51
  279.5 3.7 collective-permute-start.52
  286.5 4.1 collective-permute-done.53
  292.1 3.9 collective-permute-start.54
  297.4 3.2 collective-permute-done.55
  300.6 5.0 %collective-permute-start.56 = (f32[8,1,64]{2,1,0:T(1,128)S(1)}, f32[8,1,64]{2,1,0:T(1,128)S(1)}, u32[]{:S(2)}, u32[]{:S(2)}) collective-permute-start(f32[8,1,64]{2,1,0:T(1,128)S(1)} %get-tuple-element.130), channel_id=1, source_target_pairs={{0,16},{16,32},{32,48},{48,64},{64,80},{80,96},{96,112},{112,128},... | collective-permute-start | bytes 6152 | tf_op jit(solution)/shard_map/ppermute | solution.py:20
  307.5 3.0 collective-permute-done.57
  314.6 3.7 collective-permute-done.59
  323.0 3.4 collective-permute-done.61
  326.4 5.4 %collective-permute-start.62 = (f32[14,1,128]{2,1,0:T(1,128)S(1)}, f32[14,1,128]{2,1,0:T(1,128)S(1)}, u32[]{:S(2)}, u32[]{:S(2)}) collective-permute-start(f32[14,1,128]{2,1,0:T(1,128)S(1)} %get-tuple-element.81), channel_id=1, source_target_pairs={{0,16},{16,32},{32,48},{48,64},{64,80},{80,96},{96,112},{112,128},... | collective-permute-start | bytes 21512 | tf_op jit(solution)/shard_map/ppermute | solution.py:20
  336.9 3.6 collective-permute-start.64
  341.8 6.7 %all-reduce.8 = (f32[]{:T(128)}, f32[]{:T(128)}) all-reduce(f32[]{:T(128)} %get-tuple-element.21, f32[]{:T(128)} %get-tuple-element.20), channel_id=1, replica_groups=mesh['gx'=4,'gy_0'=8,'gy_1'=2,'gz'=16] {'gx'}, use_global_device_ids=true, to_apply=%region_5.6 | all-reduce | flops 2 | bytes 16 | tf_op jit(solution)/shard_map/psum | solution.py:30
  348.5 19.2 %all-reduce.7 = (f32[]{:T(128)}, f32[]{:T(128)}) all-reduce(f32[]{:T(128)} %get-tuple-element.26, f32[]{:T(128)} %get-tuple-element.27), channel_id=1, replica_groups=mesh['gx'=4,'gy_0'=8,'gy_1'=2,'gz'=16] {'gy_0'}, use_global_device_ids=true, to_apply=%region_6.7 | all-reduce | flops 2 | bytes 16 | tf_op jit(solution)/shard_map/psum | solution.py:30
  367.7 5.6 %all-reduce.9 = (f32[]{:T(128)}, f32[]{:T(128)}) all-reduce(f32[]{:T(128)} %get-tuple-element.24, f32[]{:T(128)} %get-tuple-element.25), channel_id=1, replica_groups=mesh['gx'=4,'gy_0'=8,'gy_1'=2,'gz'=16] {'gy_1'}, use_global_device_ids=true, to_apply=%region_7.8 | all-reduce | flops 2 | bytes 16 | tf_op jit(solution)/shard_map/psum | solution.py:30
  373.3 23.9 %all-reduce.6 = (f32[]{:T(128)}, f32[]{:T(128)}) all-reduce(f32[]{:T(128)} %get-tuple-element.28, f32[]{:T(128)} %get-tuple-element.29), channel_id=1, replica_groups=mesh['gx'=4,'gy_0'=8,'gy_1'=2,'gz'=16] {'gz'}, use_global_device_ids=true, to_apply=%region_8.9 | all-reduce | flops 2 | bytes 16 | tf_op jit(solution)/shard_map/psum | solution.py:30
  400.0 3.6 collective-permute-start.66
  405.0 3.1 collective-permute-done.67
  408.1 12.4 %collective-permute-start.68 = (f32[14,1,128]{2,1,0:T(1,128)S(1)}, f32[14,1,128]{2,1,0:T(1,128)S(1)}, u32[]{:S(2)}, u32[]{:S(2)}) collective-permute-start(f32[14,1,128]{2,1,0:T(1,128)S(1)} %get-tuple-element.79), channel_id=1, source_target_pairs={{0,16},{16,32},{32,48},{48,64},{64,80},{80,96},{96,112},{112,128},... | collective-permute-start | bytes 21512 | tf_op jit(solution)/shard_map/ppermute | solution.py:20
  429.5 4.1 collective-permute-done.71
  (282 shorter events, 110.4 us)
Async XLA Ops:
  1.6 5.2 %collective-permute-start = (f32[1,16,128]{2,1,0:T(8,128)S(1)}, f32[1,16,128]{2,1,0:T(8,128)S(1)}, u32[]{:S(2)}, u32[]{:S(2)}) collective-permute-start(f32[1,16,128]{2,1,0:T(8,128)S(1)} %get-tuple-element.104), channel_id=1, source_target_pairs={{0,256},{256,512},{512,768},{1,257},{257,513},{513,769},{2,258},{2... | collective-permute-start | bytes 24584 | tf_op jit(solution)/shard_map/ppermute | solution.py:20
  5.5 4.4 %collective-permute-start.1 = (f32[1,16,128]{2,1,0:T(8,128)S(1)}, f32[1,16,128]{2,1,0:T(8,128)S(1)}, u32[]{:S(2)}, u32[]{:S(2)}) collective-permute-start(f32[1,16,128]{2,1,0:T(8,128)S(1)} %get-tuple-element.105), channel_id=1, source_target_pairs={{256,0},{512,256},{768,512},{257,1},{513,257},{769,513},{258,2},{5... | collective-permute-start | bytes 24584 | tf_op jit(solution)/shard_map/ppermute | solution.py:23
  10.0 15.8 %collective-permute-start.2 = (f32[14,1,128]{2,1,0:T(1,128)S(1)}, f32[14,1,128]{2,1,0:T(1,128)S(1)}, u32[]{:S(2)}, u32[]{:S(2)}) collective-permute-start(f32[14,1,128]{2,1,0:T(1,128)S(1)} %get-tuple-element.89), channel_id=1, source_target_pairs={{0,16},{16,32},{32,48},{48,64},{64,80},{80,96},{96,112},{112,128},... | collective-permute-start | bytes 21512 | tf_op jit(solution)/shard_map/ppermute | solution.py:20
  15.2 11.4 %collective-permute-start.3 = (f32[14,1,128]{2,1,0:T(1,128)S(1)}, f32[14,1,128]{2,1,0:T(1,128)S(1)}, u32[]{:S(2)}, u32[]{:S(2)}) collective-permute-start(f32[14,1,128]{2,1,0:T(1,128)S(1)} %get-tuple-element.88), channel_id=1, source_target_pairs={{16,0},{32,16},{48,32},{64,48},{80,64},{96,80},{112,96},{128,112},... | collective-permute-start | bytes 21512 | tf_op jit(solution)/shard_map/ppermute | solution.py:23
  26.7 14.3 %collective-permute-start.4 = (f32[14,18,1]{2,0,1:T(8,128)S(1)}, f32[14,18,1]{2,0,1:T(8,128)S(1)}, u32[]{:S(2)}, u32[]{:S(2)}) collective-permute-start(f32[14,18,1]{2,0,1:T(8,128)S(1)} %get-tuple-element.76), channel_id=1, source_target_pairs={{0,1},{1,2},{2,3},{3,4},{4,5},{5,6},{6,7},{7,8},{8,9},{9,10},{10,1... | collective-permute-start | bytes 3032 | tf_op jit(solution)/shard_map/ppermute | solution.py:20
  28.0 13.0 %collective-permute-start.5 = (f32[14,18,1]{2,0,1:T(8,128)S(1)}, f32[14,18,1]{2,0,1:T(8,128)S(1)}, u32[]{:S(2)}, u32[]{:S(2)}) collective-permute-start(f32[14,18,1]{2,0,1:T(8,128)S(1)} %get-tuple-element.77), channel_id=1, source_target_pairs={{1,0},{2,1},{3,2},{4,3},{5,4},{6,5},{7,6},{8,7},{9,8},{10,9},{11,1... | collective-permute-start | bytes 3032 | tf_op jit(solution)/shard_map/ppermute | solution.py:23
  54.2 4.4 %collective-permute-start.7 = (f32[1,8,64]{2,1,0:T(8,128)S(1)}, f32[1,8,64]{2,1,0:T(8,128)S(1)}, u32[]{:S(2)}, u32[]{:S(2)}) collective-permute-start(f32[1,8,64]{2,1,0:T(8,128)S(1)} %get-tuple-element.147), channel_id=1, source_target_pairs={{256,0},{512,256},{768,512},{257,1},{513,257},{769,513},{258,2},{5... | collective-permute-start | bytes 6152 | tf_op jit(solution)/shard_map/ppermute | solution.py:23
  58.5 5.0 %collective-permute-start.8 = (f32[8,1,64]{2,1,0:T(1,128)S(1)}, f32[8,1,64]{2,1,0:T(1,128)S(1)}, u32[]{:S(2)}, u32[]{:S(2)}) collective-permute-start(f32[8,1,64]{2,1,0:T(1,128)S(1)} %get-tuple-element.136), channel_id=1, source_target_pairs={{0,16},{16,32},{32,48},{48,64},{64,80},{80,96},{96,112},{112,128},... | collective-permute-start | bytes 6152 | tf_op jit(solution)/shard_map/ppermute | solution.py:20
  60.5 4.9 %collective-permute-start.9 = (f32[8,1,64]{2,1,0:T(1,128)S(1)}, f32[8,1,64]{2,1,0:T(1,128)S(1)}, u32[]{:S(2)}, u32[]{:S(2)}) collective-permute-start(f32[8,1,64]{2,1,0:T(1,128)S(1)} %get-tuple-element.137), channel_id=1, source_target_pairs={{16,0},{32,16},{48,32},{64,48},{80,64},{96,80},{112,96},{128,112},... | collective-permute-start | bytes 6152 | tf_op jit(solution)/shard_map/ppermute | solution.py:23
  65.5 5.6 %collective-permute-start.10 = (f32[8,10,1]{2,0,1:T(8,128)S(1)}, f32[8,10,1]{2,0,1:T(8,128)S(1)}, u32[]{:S(2)}, u32[]{:S(2)}) collective-permute-start(f32[8,10,1]{2,0,1:T(8,128)S(1)} %get-tuple-element.128), channel_id=1, source_target_pairs={{0,1},{1,2},{2,3},{3,4},{4,5},{5,6},{6,7},{7,8},{8,9},{9,10},{10,1... | collective-permute-start | bytes 968 | tf_op jit(solution)/shard_map/ppermute | solution.py:20
  69.8 5.4 %collective-permute-start.11 = (f32[8,10,1]{2,0,1:T(8,128)S(1)}, f32[8,10,1]{2,0,1:T(8,128)S(1)}, u32[]{:S(2)}, u32[]{:S(2)}) collective-permute-start(f32[8,10,1]{2,0,1:T(8,128)S(1)} %get-tuple-element.129), channel_id=1, source_target_pairs={{1,0},{2,1},{3,2},{4,3},{5,4},{6,5},{7,6},{8,7},{9,8},{10,9},{11,1... | collective-permute-start | bytes 968 | tf_op jit(solution)/shard_map/ppermute | solution.py:23
  77.4 5.3 %collective-permute-start.13 = (f32[3,3,4,32]{3,2,1,0:T(4,128)S(1)}, f32[3,3,4,32]{3,2,1,0:T(4,128)S(1)}, u32[]{:S(2)}, u32[]{:S(2)}) collective-permute-start(f32[3,3,4,32]{3,2,1,0:T(4,128)S(1)} %pad_maximum_fusion.37), channel_id=1, source_target_pairs={{256,0},{512,256},{768,512},{257,1},{513,257},{769,513},{258,2},{5... | collective-permute-start | bytes 13832 | tf_op jit(solution)/shard_map/ppermute | solution.py:23
  78.7 4.9 %collective-permute-start.12 = (f32[3,3,4,32]{3,2,1,0:T(4,128)S(1)}, f32[3,3,4,32]{3,2,1,0:T(4,128)S(1)}, u32[]{:S(2)}, u32[]{:S(2)}) collective-permute-start(f32[3,3,4,32]{3,2,1,0:T(4,128)S(1)} %pad_maximum_fusion.37), channel_id=1, source_target_pairs={{0,256},{256,512},{512,768},{1,257},{257,513},{513,769},{2,258},{2... | collective-permute-start | bytes 13832 | tf_op jit(solution)/shard_map/ppermute | solution.py:20
  83.6 6.2 %collective-permute-start.14 = (f32[3,9,3,32]{3,2,1,0:T(4,128)S(1)}, f32[3,9,3,32]{3,2,1,0:T(4,128)S(1)}, u32[]{:S(2)}, u32[]{:S(2)}) collective-permute-start(f32[3,9,3,32]{3,2,1,0:T(4,128)S(1)} %get-tuple-element.108), channel_id=1, source_target_pairs={{0,16},{16,32},{32,48},{48,64},{64,80},{80,96},{96,112},{112,128},... | collective-permute-start | bytes 31112 | tf_op jit(solution)/shard_map/ppermute | solution.py:20
  87.9 5.5 %collective-permute-start.15 = (f32[3,9,3,32]{3,2,1,0:T(4,128)S(1)}, f32[3,9,3,32]{3,2,1,0:T(4,128)S(1)}, u32[]{:S(2)}, u32[]{:S(2)}) collective-permute-start(f32[3,9,3,32]{3,2,1,0:T(4,128)S(1)} %get-tuple-element.109), channel_id=1, source_target_pairs={{16,0},{32,16},{48,32},{64,48},{80,64},{96,80},{112,96},{128,112},... | collective-permute-start | bytes 31112 | tf_op jit(solution)/shard_map/ppermute | solution.py:23
  93.5 8.6 %collective-permute-start.16 = (f32[3,9,10,3]{3,2,1,0:T(8,128)S(1)}, f32[3,9,10,3]{3,2,1,0:T(8,128)S(1)}, u32[]{:S(2)}, u32[]{:S(2)}) collective-permute-start(f32[3,9,10,3]{3,2,1,0:T(8,128)S(1)} %get-tuple-element.64), channel_id=1, source_target_pairs={{0,1},{1,2},{2,3},{3,4},{4,5},{5,6},{6,7},{7,8},{8,9},{9,10},{10,1... | collective-permute-start | bytes 9728 | tf_op jit(solution)/shard_map/ppermute | solution.py:20
  98.8 8.7 %collective-permute-start.17 = (f32[3,9,10,3]{3,2,1,0:T(8,128)S(1)}, f32[3,9,10,3]{3,2,1,0:T(8,128)S(1)}, u32[]{:S(2)}, u32[]{:S(2)}) collective-permute-start(f32[3,9,10,3]{3,2,1,0:T(8,128)S(1)} %get-tuple-element.65), channel_id=1, source_target_pairs={{1,0},{2,1},{3,2},{4,3},{5,4},{6,5},{7,6},{8,7},{9,8},{10,9},{11,1... | collective-permute-start | bytes 9728 | tf_op jit(solution)/shard_map/ppermute | solution.py:23
  109.0 5.2 %collective-permute-start.18 = (f32[1,8,64]{2,1,0:T(8,128)S(1)}, f32[1,8,64]{2,1,0:T(8,128)S(1)}, u32[]{:S(2)}, u32[]{:S(2)}) collective-permute-start(f32[1,8,64]{2,1,0:T(8,128)S(1)} %get-tuple-element.142), channel_id=1, source_target_pairs={{0,256},{256,512},{512,768},{1,257},{257,513},{513,769},{2,258},{2... | collective-permute-start | bytes 6152 | tf_op jit(solution)/shard_map/ppermute | solution.py:20
  112.9 4.4 %collective-permute-start.19 = (f32[1,8,64]{2,1,0:T(8,128)S(1)}, f32[1,8,64]{2,1,0:T(8,128)S(1)}, u32[]{:S(2)}, u32[]{:S(2)}) collective-permute-start(f32[1,8,64]{2,1,0:T(8,128)S(1)} %get-tuple-element.143), channel_id=1, source_target_pairs={{256,0},{512,256},{768,512},{257,1},{513,257},{769,513},{258,2},{5... | collective-permute-start | bytes 6152 | tf_op jit(solution)/shard_map/ppermute | solution.py:23
  117.3 7.5 %collective-permute-start.20 = (f32[8,1,64]{2,1,0:T(1,128)S(1)}, f32[8,1,64]{2,1,0:T(1,128)S(1)}, u32[]{:S(2)}, u32[]{:S(2)}) collective-permute-start(f32[8,1,64]{2,1,0:T(1,128)S(1)} %get-tuple-element.134), channel_id=1, source_target_pairs={{0,16},{16,32},{32,48},{48,64},{64,80},{80,96},{96,112},{112,128},... | collective-permute-start | bytes 6152 | tf_op jit(solution)/shard_map/ppermute | solution.py:20
  122.9 4.9 %collective-permute-start.21 = (f32[8,1,64]{2,1,0:T(1,128)S(1)}, f32[8,1,64]{2,1,0:T(1,128)S(1)}, u32[]{:S(2)}, u32[]{:S(2)}) collective-permute-start(f32[8,1,64]{2,1,0:T(1,128)S(1)} %get-tuple-element.135), channel_id=1, source_target_pairs={{16,0},{32,16},{48,32},{64,48},{80,64},{96,80},{112,96},{128,112},... | collective-permute-start | bytes 6152 | tf_op jit(solution)/shard_map/ppermute | solution.py:23
  127.9 6.2 %collective-permute-start.22 = (f32[8,10,1]{2,0,1:T(8,128)S(1)}, f32[8,10,1]{2,0,1:T(8,128)S(1)}, u32[]{:S(2)}, u32[]{:S(2)}) collective-permute-start(f32[8,10,1]{2,0,1:T(8,128)S(1)} %get-tuple-element.123), channel_id=1, source_target_pairs={{0,1},{1,2},{2,3},{3,4},{4,5},{5,6},{6,7},{7,8},{8,9},{9,10},{10,1... | collective-permute-start | bytes 968 | tf_op jit(solution)/shard_map/ppermute | solution.py:20
  132.8 5.3 %collective-permute-start.23 = (f32[8,10,1]{2,0,1:T(8,128)S(1)}, f32[8,10,1]{2,0,1:T(8,128)S(1)}, u32[]{:S(2)}, u32[]{:S(2)}) collective-permute-start(f32[8,10,1]{2,0,1:T(8,128)S(1)} %get-tuple-element.124), channel_id=1, source_target_pairs={{1,0},{2,1},{3,2},{4,3},{5,4},{6,5},{7,6},{8,7},{9,8},{10,9},{11,1... | collective-permute-start | bytes 968 | tf_op jit(solution)/shard_map/ppermute | solution.py:23
  142.0 4.7 %collective-permute-start.25 = (f32[1,16,128]{2,1,0:T(8,128)S(1)}, f32[1,16,128]{2,1,0:T(8,128)S(1)}, u32[]{:S(2)}, u32[]{:S(2)}) collective-permute-start(f32[1,16,128]{2,1,0:T(8,128)S(1)} %get-tuple-element.103), channel_id=1, source_target_pairs={{256,0},{512,256},{768,512},{257,1},{513,257},{769,513},{258,2},{5... | collective-permute-start | bytes 24584 | tf_op jit(solution)/shard_map/ppermute | solution.py:23
  146.8 6.5 %collective-permute-start.26 = (f32[14,1,128]{2,1,0:T(1,128)S(1)}, f32[14,1,128]{2,1,0:T(1,128)S(1)}, u32[]{:S(2)}, u32[]{:S(2)}) collective-permute-start(f32[14,1,128]{2,1,0:T(1,128)S(1)} %get-tuple-element.87), channel_id=1, source_target_pairs={{0,16},{16,32},{32,48},{48,64},{64,80},{80,96},{96,112},{112,128},... | collective-permute-start | bytes 21512 | tf_op jit(solution)/shard_map/ppermute | solution.py:20
  151.3 5.0 %collective-permute-start.27 = (f32[14,1,128]{2,1,0:T(1,128)S(1)}, f32[14,1,128]{2,1,0:T(1,128)S(1)}, u32[]{:S(2)}, u32[]{:S(2)}) collective-permute-start(f32[14,1,128]{2,1,0:T(1,128)S(1)} %get-tuple-element.86), channel_id=1, source_target_pairs={{16,0},{32,16},{48,32},{64,48},{80,64},{96,80},{112,96},{128,112},... | collective-permute-start | bytes 21512 | tf_op jit(solution)/shard_map/ppermute | solution.py:23
  156.4 5.9 %collective-permute-start.28 = (f32[14,18,1]{2,0,1:T(8,128)S(1)}, f32[14,18,1]{2,0,1:T(8,128)S(1)}, u32[]{:S(2)}, u32[]{:S(2)}) collective-permute-start(f32[14,18,1]{2,0,1:T(8,128)S(1)} %get-tuple-element.74), channel_id=1, source_target_pairs={{0,1},{1,2},{2,3},{3,4},{4,5},{5,6},{6,7},{7,8},{8,9},{9,10},{10,1... | collective-permute-start | bytes 3032 | tf_op jit(solution)/shard_map/ppermute | solution.py:20
  160.1 7.3 %collective-permute-start.29 = (f32[14,18,1]{2,0,1:T(8,128)S(1)}, f32[14,18,1]{2,0,1:T(8,128)S(1)}, u32[]{:S(2)}, u32[]{:S(2)}) collective-permute-start(f32[14,18,1]{2,0,1:T(8,128)S(1)} %get-tuple-element.75), channel_id=1, source_target_pairs={{1,0},{2,1},{3,2},{4,3},{5,4},{6,5},{7,6},{8,7},{9,8},{10,9},{11,1... | collective-permute-start | bytes 3032 | tf_op jit(solution)/shard_map/ppermute | solution.py:23
  169.9 4.8 %collective-permute-start.31 = (f32[1,16,128]{2,1,0:T(8,128)S(1)}, f32[1,16,128]{2,1,0:T(8,128)S(1)}, u32[]{:S(2)}, u32[]{:S(2)}) collective-permute-start(f32[1,16,128]{2,1,0:T(8,128)S(1)} %get-tuple-element.101), channel_id=1, source_target_pairs={{256,0},{512,256},{768,512},{257,1},{513,257},{769,513},{258,2},{5... | collective-permute-start | bytes 24584 | tf_op jit(solution)/shard_map/ppermute | solution.py:23
  174.7 6.9 %collective-permute-start.32 = (f32[14,1,128]{2,1,0:T(1,128)S(1)}, f32[14,1,128]{2,1,0:T(1,128)S(1)}, u32[]{:S(2)}, u32[]{:S(2)}) collective-permute-start(f32[14,1,128]{2,1,0:T(1,128)S(1)} %get-tuple-element.85), channel_id=1, source_target_pairs={{0,16},{16,32},{32,48},{48,64},{64,80},{80,96},{96,112},{112,128},... | collective-permute-start | bytes 21512 | tf_op jit(solution)/shard_map/ppermute | solution.py:20
  179.7 5.0 %collective-permute-start.33 = (f32[14,1,128]{2,1,0:T(1,128)S(1)}, f32[14,1,128]{2,1,0:T(1,128)S(1)}, u32[]{:S(2)}, u32[]{:S(2)}) collective-permute-start(f32[14,1,128]{2,1,0:T(1,128)S(1)} %get-tuple-element.84), channel_id=1, source_target_pairs={{16,0},{32,16},{48,32},{64,48},{80,64},{96,80},{112,96},{128,112},... | collective-permute-start | bytes 21512 | tf_op jit(solution)/shard_map/ppermute | solution.py:23
  184.7 7.4 %collective-permute-start.34 = (f32[14,18,1]{2,0,1:T(8,128)S(1)}, f32[14,18,1]{2,0,1:T(8,128)S(1)}, u32[]{:S(2)}, u32[]{:S(2)}) collective-permute-start(f32[14,18,1]{2,0,1:T(8,128)S(1)} %get-tuple-element.72), channel_id=1, source_target_pairs={{0,1},{1,2},{2,3},{3,4},{4,5},{5,6},{6,7},{7,8},{8,9},{9,10},{10,1... | collective-permute-start | bytes 3032 | tf_op jit(solution)/shard_map/ppermute | solution.py:20
  189.9 6.9 %collective-permute-start.35 = (f32[14,18,1]{2,0,1:T(8,128)S(1)}, f32[14,18,1]{2,0,1:T(8,128)S(1)}, u32[]{:S(2)}, u32[]{:S(2)}) collective-permute-start(f32[14,18,1]{2,0,1:T(8,128)S(1)} %get-tuple-element.73), channel_id=1, source_target_pairs={{1,0},{2,1},{3,2},{4,3},{5,4},{6,5},{7,6},{8,7},{9,8},{10,9},{11,1... | collective-permute-start | bytes 3032 | tf_op jit(solution)/shard_map/ppermute | solution.py:23
  199.3 5.0 %collective-permute-start.37 = (f32[1,16,128]{2,1,0:T(8,128)S(1)}, f32[1,16,128]{2,1,0:T(8,128)S(1)}, u32[]{:S(2)}, u32[]{:S(2)}) collective-permute-start(f32[1,16,128]{2,1,0:T(8,128)S(1)} %get-tuple-element.99), channel_id=1, source_target_pairs={{256,0},{512,256},{768,512},{257,1},{513,257},{769,513},{258,2},{5... | collective-permute-start | bytes 24584 | tf_op jit(solution)/shard_map/ppermute | solution.py:23
  204.3 7.1 %collective-permute-start.38 = (f32[14,1,128]{2,1,0:T(1,128)S(1)}, f32[14,1,128]{2,1,0:T(1,128)S(1)}, u32[]{:S(2)}, u32[]{:S(2)}) collective-permute-start(f32[14,1,128]{2,1,0:T(1,128)S(1)} %get-tuple-element.83), channel_id=1, source_target_pairs={{0,16},{16,32},{32,48},{48,64},{64,80},{80,96},{96,112},{112,128},... | collective-permute-start | bytes 21512 | tf_op jit(solution)/shard_map/ppermute | solution.py:20
  209.4 5.0 %collective-permute-start.39 = (f32[14,1,128]{2,1,0:T(1,128)S(1)}, f32[14,1,128]{2,1,0:T(1,128)S(1)}, u32[]{:S(2)}, u32[]{:S(2)}) collective-permute-start(f32[14,1,128]{2,1,0:T(1,128)S(1)} %get-tuple-element.82), channel_id=1, source_target_pairs={{16,0},{32,16},{48,32},{64,48},{80,64},{96,80},{112,96},{128,112},... | collective-permute-start | bytes 21512 | tf_op jit(solution)/shard_map/ppermute | solution.py:23
  214.5 6.7 %collective-permute-start.40 = (f32[14,18,1]{2,0,1:T(8,128)S(1)}, f32[14,18,1]{2,0,1:T(8,128)S(1)}, u32[]{:S(2)}, u32[]{:S(2)}) collective-permute-start(f32[14,18,1]{2,0,1:T(8,128)S(1)} %get-tuple-element.70), channel_id=1, source_target_pairs={{0,1},{1,2},{2,3},{3,4},{4,5},{5,6},{6,7},{7,8},{8,9},{9,10},{10,1... | collective-permute-start | bytes 3032 | tf_op jit(solution)/shard_map/ppermute | solution.py:20
  218.9 6.6 %collective-permute-start.41 = (f32[14,18,1]{2,0,1:T(8,128)S(1)}, f32[14,18,1]{2,0,1:T(8,128)S(1)}, u32[]{:S(2)}, u32[]{:S(2)}) collective-permute-start(f32[14,18,1]{2,0,1:T(8,128)S(1)} %get-tuple-element.71), channel_id=1, source_target_pairs={{1,0},{2,1},{3,2},{4,3},{5,4},{6,5},{7,6},{8,7},{9,8},{10,9},{11,1... | collective-permute-start | bytes 3032 | tf_op jit(solution)/shard_map/ppermute | solution.py:23
  239.0 4.7 %collective-permute-start.43 = (f32[1,8,64]{2,1,0:T(8,128)S(1)}, f32[1,8,64]{2,1,0:T(8,128)S(1)}, u32[]{:S(2)}, u32[]{:S(2)}) collective-permute-start(f32[1,8,64]{2,1,0:T(8,128)S(1)} %get-tuple-element.141), channel_id=1, source_target_pairs={{256,0},{512,256},{768,512},{257,1},{513,257},{769,513},{258,2},{5... | collective-permute-start | bytes 6152 | tf_op jit(solution)/shard_map/ppermute | solution.py:23
  243.7 6.6 %collective-permute-start.44 = (f32[8,1,64]{2,1,0:T(1,128)S(1)}, f32[8,1,64]{2,1,0:T(1,128)S(1)}, u32[]{:S(2)}, u32[]{:S(2)}) collective-permute-start(f32[8,1,64]{2,1,0:T(1,128)S(1)} %get-tuple-element.132), channel_id=1, source_target_pairs={{0,16},{16,32},{32,48},{48,64},{64,80},{80,96},{96,112},{112,128},... | collective-permute-start | bytes 6152 | tf_op jit(solution)/shard_map/ppermute | solution.py:20
  248.3 4.9 %collective-permute-start.45 = (f32[8,1,64]{2,1,0:T(1,128)S(1)}, f32[8,1,64]{2,1,0:T(1,128)S(1)}, u32[]{:S(2)}, u32[]{:S(2)}) collective-permute-start(f32[8,1,64]{2,1,0:T(1,128)S(1)} %get-tuple-element.133), channel_id=1, source_target_pairs={{16,0},{32,16},{48,32},{64,48},{80,64},{96,80},{112,96},{128,112},... | collective-permute-start | bytes 6152 | tf_op jit(solution)/shard_map/ppermute | solution.py:23
  253.3 4.9 %collective-permute-start.46 = (f32[8,10,1]{2,0,1:T(8,128)S(1)}, f32[8,10,1]{2,0,1:T(8,128)S(1)}, u32[]{:S(2)}, u32[]{:S(2)}) collective-permute-start(f32[8,10,1]{2,0,1:T(8,128)S(1)} %get-tuple-element.118), channel_id=1, source_target_pairs={{0,1},{1,2},{2,3},{3,4},{4,5},{5,6},{6,7},{7,8},{8,9},{9,10},{10,1... | collective-permute-start | bytes 968 | tf_op jit(solution)/shard_map/ppermute | solution.py:20
  257.0 5.1 %collective-permute-start.47 = (f32[8,10,1]{2,0,1:T(8,128)S(1)}, f32[8,10,1]{2,0,1:T(8,128)S(1)}, u32[]{:S(2)}, u32[]{:S(2)}) collective-permute-start(f32[8,10,1]{2,0,1:T(8,128)S(1)} %get-tuple-element.119), channel_id=1, source_target_pairs={{1,0},{2,1},{3,2},{4,3},{5,4},{6,5},{7,6},{8,7},{9,8},{10,9},{11,1... | collective-permute-start | bytes 968 | tf_op jit(solution)/shard_map/ppermute | solution.py:23
  263.3 5.3 %collective-permute-start.49 = (f32[3,3,4,32]{3,2,1,0:T(4,128)S(1)}, f32[3,3,4,32]{3,2,1,0:T(4,128)S(1)}, u32[]{:S(2)}, u32[]{:S(2)}) collective-permute-start(f32[3,3,4,32]{3,2,1,0:T(4,128)S(1)} %pad_maximum_fusion.36), channel_id=1, source_target_pairs={{256,0},{512,256},{768,512},{257,1},{513,257},{769,513},{258,2},{5... | collective-permute-start | bytes 13832 | tf_op jit(solution)/shard_map/ppermute | solution.py:23
  264.6 4.9 %collective-permute-start.48 = (f32[3,3,4,32]{3,2,1,0:T(4,128)S(1)}, f32[3,3,4,32]{3,2,1,0:T(4,128)S(1)}, u32[]{:S(2)}, u32[]{:S(2)}) collective-permute-start(f32[3,3,4,32]{3,2,1,0:T(4,128)S(1)} %pad_maximum_fusion.36), channel_id=1, source_target_pairs={{0,256},{256,512},{512,768},{1,257},{257,513},{513,769},{2,258},{2... | collective-permute-start | bytes 13832 | tf_op jit(solution)/shard_map/ppermute | solution.py:20
  269.5 6.2 %collective-permute-start.50 = (f32[3,9,3,32]{3,2,1,0:T(4,128)S(1)}, f32[3,9,3,32]{3,2,1,0:T(4,128)S(1)}, u32[]{:S(2)}, u32[]{:S(2)}) collective-permute-start(f32[3,9,3,32]{3,2,1,0:T(4,128)S(1)} %get-tuple-element.106), channel_id=1, source_target_pairs={{0,16},{16,32},{32,48},{48,64},{64,80},{80,96},{96,112},{112,128},... | collective-permute-start | bytes 31112 | tf_op jit(solution)/shard_map/ppermute | solution.py:20
  273.8 5.5 %collective-permute-start.51 = (f32[3,9,3,32]{3,2,1,0:T(4,128)S(1)}, f32[3,9,3,32]{3,2,1,0:T(4,128)S(1)}, u32[]{:S(2)}, u32[]{:S(2)}) collective-permute-start(f32[3,9,3,32]{3,2,1,0:T(4,128)S(1)} %get-tuple-element.107), channel_id=1, source_target_pairs={{16,0},{32,16},{48,32},{64,48},{80,64},{96,80},{112,96},{128,112},... | collective-permute-start | bytes 31112 | tf_op jit(solution)/shard_map/ppermute | solution.py:23
  279.5 7.0 %collective-permute-start.52 = (f32[3,9,10,3]{3,2,1,0:T(8,128)S(1)}, f32[3,9,10,3]{3,2,1,0:T(8,128)S(1)}, u32[]{:S(2)}, u32[]{:S(2)}) collective-permute-start(f32[3,9,10,3]{3,2,1,0:T(8,128)S(1)} %get-tuple-element.59), channel_id=1, source_target_pairs={{0,1},{1,2},{2,3},{3,4},{4,5},{5,6},{6,7},{7,8},{8,9},{9,10},{10,1... | collective-permute-start | bytes 9728 | tf_op jit(solution)/shard_map/ppermute | solution.py:20
  283.1 7.5 %collective-permute-start.53 = (f32[3,9,10,3]{3,2,1,0:T(8,128)S(1)}, f32[3,9,10,3]{3,2,1,0:T(8,128)S(1)}, u32[]{:S(2)}, u32[]{:S(2)}) collective-permute-start(f32[3,9,10,3]{3,2,1,0:T(8,128)S(1)} %get-tuple-element.60), channel_id=1, source_target_pairs={{1,0},{2,1},{3,2},{4,3},{5,4},{6,5},{7,6},{8,7},{9,8},{10,9},{11,1... | collective-permute-start | bytes 9728 | tf_op jit(solution)/shard_map/ppermute | solution.py:23
  292.1 5.2 %collective-permute-start.54 = (f32[1,8,64]{2,1,0:T(8,128)S(1)}, f32[1,8,64]{2,1,0:T(8,128)S(1)}, u32[]{:S(2)}, u32[]{:S(2)}) collective-permute-start(f32[1,8,64]{2,1,0:T(8,128)S(1)} %get-tuple-element.138), channel_id=1, source_target_pairs={{0,256},{256,512},{512,768},{1,257},{257,513},{513,769},{2,258},{2... | collective-permute-start | bytes 6152 | tf_op jit(solution)/shard_map/ppermute | solution.py:20
  296.1 4.5 %collective-permute-start.55 = (f32[1,8,64]{2,1,0:T(8,128)S(1)}, f32[1,8,64]{2,1,0:T(8,128)S(1)}, u32[]{:S(2)}, u32[]{:S(2)}) collective-permute-start(f32[1,8,64]{2,1,0:T(8,128)S(1)} %get-tuple-element.139), channel_id=1, source_target_pairs={{256,0},{512,256},{768,512},{257,1},{513,257},{769,513},{258,2},{5... | collective-permute-start | bytes 6152 | tf_op jit(solution)/shard_map/ppermute | solution.py:23
  300.6 6.9 %collective-permute-start.56 = (f32[8,1,64]{2,1,0:T(1,128)S(1)}, f32[8,1,64]{2,1,0:T(1,128)S(1)}, u32[]{:S(2)}, u32[]{:S(2)}) collective-permute-start(f32[8,1,64]{2,1,0:T(1,128)S(1)} %get-tuple-element.130), channel_id=1, source_target_pairs={{0,16},{16,32},{32,48},{48,64},{64,80},{80,96},{96,112},{112,128},... | collective-permute-start | bytes 6152 | tf_op jit(solution)/shard_map/ppermute | solution.py:20
  305.5 4.9 %collective-permute-start.57 = (f32[8,1,64]{2,1,0:T(1,128)S(1)}, f32[8,1,64]{2,1,0:T(1,128)S(1)}, u32[]{:S(2)}, u32[]{:S(2)}) collective-permute-start(f32[8,1,64]{2,1,0:T(1,128)S(1)} %get-tuple-element.131), channel_id=1, source_target_pairs={{16,0},{32,16},{48,32},{64,48},{80,64},{96,80},{112,96},{128,112},... | collective-permute-start | bytes 6152 | tf_op jit(solution)/shard_map/ppermute | solution.py:23
  313.3 5.0 %collective-permute-start.59 = (f32[8,10,1]{2,0,1:T(8,128)S(1)}, f32[8,10,1]{2,0,1:T(8,128)S(1)}, u32[]{:S(2)}, u32[]{:S(2)}) collective-permute-start(f32[8,10,1]{2,0,1:T(8,128)S(1)} %get-tuple-element.114), channel_id=1, source_target_pairs={{1,0},{2,1},{3,2},{4,3},{5,4},{6,5},{7,6},{8,7},{9,8},{10,9},{11,1... | collective-permute-start | bytes 968 | tf_op jit(solution)/shard_map/ppermute | solution.py:23
  321.7 4.7 %collective-permute-start.61 = (f32[1,16,128]{2,1,0:T(8,128)S(1)}, f32[1,16,128]{2,1,0:T(8,128)S(1)}, u32[]{:S(2)}, u32[]{:S(2)}) collective-permute-start(f32[1,16,128]{2,1,0:T(8,128)S(1)} %get-tuple-element.96), channel_id=1, source_target_pairs={{256,0},{512,256},{768,512},{257,1},{513,257},{769,513},{258,2},{5... | collective-permute-start | bytes 24584 | tf_op jit(solution)/shard_map/ppermute | solution.py:23
  326.4 7.3 %collective-permute-start.62 = (f32[14,1,128]{2,1,0:T(1,128)S(1)}, f32[14,1,128]{2,1,0:T(1,128)S(1)}, u32[]{:S(2)}, u32[]{:S(2)}) collective-permute-start(f32[14,1,128]{2,1,0:T(1,128)S(1)} %get-tuple-element.81), channel_id=1, source_target_pairs={{0,16},{16,32},{32,48},{48,64},{64,80},{80,96},{96,112},{112,128},... | collective-permute-start | bytes 21512 | tf_op jit(solution)/shard_map/ppermute | solution.py:20
  331.8 5.0 %collective-permute-start.63 = (f32[14,1,128]{2,1,0:T(1,128)S(1)}, f32[14,1,128]{2,1,0:T(1,128)S(1)}, u32[]{:S(2)}, u32[]{:S(2)}) collective-permute-start(f32[14,1,128]{2,1,0:T(1,128)S(1)} %get-tuple-element.80), channel_id=1, source_target_pairs={{16,0},{32,16},{48,32},{64,48},{80,64},{96,80},{112,96},{128,112},... | collective-permute-start | bytes 21512 | tf_op jit(solution)/shard_map/ppermute | solution.py:23
  336.9 61.7 %collective-permute-start.64 = (f32[14,18,1]{2,0,1:T(8,128)S(1)}, f32[14,18,1]{2,0,1:T(8,128)S(1)}, u32[]{:S(2)}, u32[]{:S(2)}) collective-permute-start(f32[14,18,1]{2,0,1:T(8,128)S(1)} %get-tuple-element.68), channel_id=1, source_target_pairs={{0,1},{1,2},{2,3},{3,4},{4,5},{5,6},{6,7},{7,8},{8,9},{9,10},{10,1... | collective-permute-start | bytes 3032 | tf_op jit(solution)/shard_map/ppermute | solution.py:20
  340.5 58.0 %collective-permute-start.65 = (f32[14,18,1]{2,0,1:T(8,128)S(1)}, f32[14,18,1]{2,0,1:T(8,128)S(1)}, u32[]{:S(2)}, u32[]{:S(2)}) collective-permute-start(f32[14,18,1]{2,0,1:T(8,128)S(1)} %get-tuple-element.69), channel_id=1, source_target_pairs={{1,0},{2,1},{3,2},{4,3},{5,4},{6,5},{7,6},{8,7},{9,8},{10,9},{11,1... | collective-permute-start | bytes 3032 | tf_op jit(solution)/shard_map/ppermute | solution.py:23
  400.0 4.9 %collective-permute-start.66 = (f32[1,16,128]{2,1,0:T(8,128)S(1)}, f32[1,16,128]{2,1,0:T(8,128)S(1)}, u32[]{:S(2)}, u32[]{:S(2)}) collective-permute-start(f32[1,16,128]{2,1,0:T(8,128)S(1)} %get-tuple-element.92), channel_id=1, source_target_pairs={{0,256},{256,512},{512,768},{1,257},{257,513},{513,769},{2,258},{2... | collective-permute-start | bytes 24584 | tf_op jit(solution)/shard_map/ppermute | solution.py:20
  403.7 4.4 %collective-permute-start.67 = (f32[1,16,128]{2,1,0:T(8,128)S(1)}, f32[1,16,128]{2,1,0:T(8,128)S(1)}, u32[]{:S(2)}, u32[]{:S(2)}) collective-permute-start(f32[1,16,128]{2,1,0:T(8,128)S(1)} %get-tuple-element.93), channel_id=1, source_target_pairs={{256,0},{512,256},{768,512},{257,1},{513,257},{769,513},{258,2},{5... | collective-permute-start | bytes 24584 | tf_op jit(solution)/shard_map/ppermute | solution.py:23
  408.1 14.4 %collective-permute-start.68 = (f32[14,1,128]{2,1,0:T(1,128)S(1)}, f32[14,1,128]{2,1,0:T(1,128)S(1)}, u32[]{:S(2)}, u32[]{:S(2)}) collective-permute-start(f32[14,1,128]{2,1,0:T(1,128)S(1)} %get-tuple-element.79), channel_id=1, source_target_pairs={{0,16},{16,32},{32,48},{48,64},{64,80},{80,96},{96,112},{112,128},... | collective-permute-start | bytes 21512 | tf_op jit(solution)/shard_map/ppermute | solution.py:20
  420.5 5.0 %collective-permute-start.69 = (f32[14,1,128]{2,1,0:T(1,128)S(1)}, f32[14,1,128]{2,1,0:T(1,128)S(1)}, u32[]{:S(2)}, u32[]{:S(2)}) collective-permute-start(f32[14,1,128]{2,1,0:T(1,128)S(1)} %get-tuple-element.78), channel_id=1, source_target_pairs={{16,0},{32,16},{48,32},{64,48},{80,64},{96,80},{112,96},{128,112},... | collective-permute-start | bytes 21512 | tf_op jit(solution)/shard_map/ppermute | solution.py:23
  427.2 6.3 %collective-permute-start.71 = (f32[14,18,1]{2,0,1:T(8,128)S(1)}, f32[14,18,1]{2,0,1:T(8,128)S(1)}, u32[]{:S(2)}, u32[]{:S(2)}) collective-permute-start(f32[14,18,1]{2,0,1:T(8,128)S(1)} %get-tuple-element.67), channel_id=1, source_target_pairs={{1,0},{2,1},{3,2},{4,3},{5,4},{6,5},{7,6},{8,7},{9,8},{10,9},{11,1... | collective-permute-start | bytes 3032 | tf_op jit(solution)/shard_map/ppermute | solution.py:23
  (10 other events, 34.9 us)
where the time goes:
time: 438 us; the launch traced here: 435 us
  starting transfers between devices  206 us (47%)
  waiting for transfers between devices  119 us (27%)
  blocking collectives  55.4 us (13%)
  local copies, waits for them, and re-layouts  30 us (7%)
  other arithmetic  21 us (5%)
    ppermute x36, starting transfers between devices, with_halo(): lax.ppermute(lax.slice_in_dim(block, block.shape[dim] - width, None, axis...  142 us
    ppermute x36, waiting for transfers between devices, with_halo(): lax.ppermute(lax.slice_in_dim(block, 0, width, axis=dim), axis, backward)  109 us
    ppermute x36, starting transfers between devices, with_halo(): lax.ppermute(lax.slice_in_dim(block, 0, width, axis=dim), axis, backward)  64.1 us
    psum x4, blocking collectives, over_axes(): array = lax.psum(array, axis)  55.4 us
    reshape x5, local copies, waits for them, and re-layouts, restrict(): values.reshape(extent[0] // 2, 2, extent[1] // 2, 2, extent[2] // 2, 2)  25.2 us
    reduce_sum x6, other arithmetic, restrict(): return 0.5 * grouped.sum(axis=(1, 3, 5))  10.3 us
    ppermute x36, waiting for transfers between devices, with_halo(): lax.ppermute(lax.slice_in_dim(block, block.shape[dim] - width, None, axis...  9.57 us
  transfers between devices with their start and end apart: 72, of which 40 were waited for; matrix products, arithmetic and copies ran while one was open for 3% of the time, Pallas kernels for 0%

commit v1 on v0

v1 whole, which is shorter than its diff:
```python
import functools

import jax
import jax.numpy as jnp
from jax import lax
from jax.experimental import pallas as pl
from jax.experimental.pallas import tpu as pltpu
from jax.sharding import PartitionSpec as P

MESH = pl.DeviceIdType.MESH
F32 = jnp.float32
BF16 = jnp.bfloat16

BX, BY, BZ = 12, 16, 128
CX, CY, CZ = 3, 4, 32
HX = 5
LX = BX + 2 * HX
LY = 32
FINE = [
    (dx, dy, dz)
    for dx in (-1, 0, 1)
    for dy in (-1, 0, 1)
    for dz in (-1, 0, 1)
    if (dx, dy, dz) != (0, 0, 0)
]
DEEP = [
    (dx, dy, dz)
    for dx in (-2, -1, 0, 1, 2)
    for dy in (-1, 0, 1)
    for dz in (-1, 0, 1)
    if (dx, dy, dz) != (0, 0, 0)
]


def iota(shape, axis):
    return lax.broadcasted_iota(jnp.int32, shape, axis)


def split(values):
    high = values.astype(BF16)
    rest = values - high.astype(F32)
    middle = rest.astype(BF16)
    low = (rest - middle.astype(F32)).astype(BF16)
    return high, middle, low


def select_dot(values, table):
    high, middle, low = split(values)
    dot = functools.partial(jnp.dot, preferred_element_type=F32)
    return dot(low, table) + dot(middle, table) + dot(high, table)


def ones_where(condition):
    return jnp.where(condition, 1.0, 0.0).astype(BF16)


def wrapped(lane, size):
    return jnp.where(lane < size * 3 // 4, lane, lane - size)


def around(plane):
    rows, lanes = plane.shape[-2:]
    axis = plane.ndim - 2
    plane = plane + pltpu.roll(plane, 1, axis) + pltpu.roll(plane, rows - 1, axis)
    return plane + pltpu.roll(plane, 1, axis + 1) + pltpu.roll(plane, lanes - 1, axis + 1)


def loop(count, unroll, body):
    def step(i, carry):
        body(i)
        return carry

    lax.fori_loop(0, count, step, 0, unroll=unroll)


def kernel(
    sizes,
    g_hbm, c_hbm,
    p_out, image_out, mw_out, nw_out, sums_out,
    own, ext, packed, halo, coarse_own, coarse_ext,
    wide, inv0, e0, rest0, inv1, g1, e1, inv2, coarse,
    t_fine, t_mid, p_mid, p_fine,
    m_pack, m_unpack, m_r0, m_r1, m_p1, m_p0,
    load_sem, fine_send, fine_recv, deep_send, deep_recv,
):
    nx, ny, nz = sizes
    gx, gy, gz = lax.axis_index("gx"), lax.axis_index("gy"), lax.axis_index("gz")

    def exists(d):
        checks = []
        for delta, at, count in zip(d, (gx, gy, gz), sizes):
            if delta < 0:
                checks.append(at >= -delta)
            if delta > 0:
                checks.append(at < count - delta)
        return functools.reduce(jnp.logical_and, checks)

    def device(d):
        return (gx + d[0], gy + d[1], gz + d[2])

    loads = [
        pltpu.make_async_copy(g_hbm, own.at[0], load_sem.at[0]),
        pltpu.make_async_copy(c_hbm, own.at[1], load_sem.at[1]),
    ]
    for load in loads:
        load.start()

    ext[...] = jnp.zeros_like(ext)
    halo[...] = jnp.zeros_like(halo)
    coarse_ext[...] = jnp.zeros_like(coarse_ext)

    barrier = pltpu.get_barrier_semaphore()
    for d in DEEP:
        @pl.when(exists(d))
        def _(d=d):
            pl.semaphore_signal(barrier, inc=1, device_id=device(d), device_id_type=MESH)

    row, col = iota((BZ, 2 * BZ), 0), iota((BZ, 2 * BZ), 1)
    m_pack[...] = ones_where(row == jnp.where(col < BZ, col % 8, 120 + col % 8))
    row, col = iota((2 * BZ, BZ), 0), iota((2 * BZ, BZ), 1)
    m_unpack[...] = ones_where(col == jnp.where(row < BZ, 120 + row % 8, row % 8))
    m_r0[...] = ones_where(col == (jnp.where(row < 192, row, row - 256) >> 1) % 128)
    row, col = iota((BZ, BZ), 0), iota((BZ, BZ), 1)
    m_r1[...] = ones_where(jnp.logical_and(row < 64, (row >> 1) == col % 32))
    m_p1[...] = ones_where(row == (wrapped(col, 128) >> 1) % 128)
    row, col = iota((BZ, 2 * BZ), 0), iota((BZ, 2 * BZ), 1)
    m_p0[...] = ones_where(row == (wrapped(col, 256) >> 1) % 128)

    def pack(field):
        values = own[field].reshape(BX * BY, BZ)
        spread = select_dot(values, m_pack[...]).reshape(BX, BY, 2 * BZ)
        lane, row = iota((BX, BY, 2 * BZ), 2), iota((BX, BY, 2 * BZ), 1)
        spread = jnp.where((lane % 128) // 8 == row, spread, 0.0)
        flat = jnp.sum(spread, axis=1, keepdims=True)
        packed[0, field] = flat[:, :, :BZ]
        packed[1, field] = flat[:, :, BZ:]

    def fine_copies(first, count):
        fields = pl.ds(first, count)
        for n, (dx, dy, dz) in enumerate(FINE):
            source = {-1: pl.ds(0, HX), 0: pl.ds(0, BX), 1: pl.ds(BX - HX, HX)}[dx]
            target = {-1: pl.ds(HX + BX, HX), 0: pl.ds(HX, BX), 1: pl.ds(0, HX)}[dx]
            if dz == 0:
                rows = {-1: pl.ds(0, 8), 0: pl.ds(0, 16), 1: pl.ds(8, 8)}[dy]
                to = {-1: pl.ds(24, 8), 0: pl.ds(8, 16), 1: pl.ds(0, 8)}[dy]
                src, dst = own.at[fields, source, rows], ext.at[fields, target, to]
            else:
                src = packed.at[(dz + 1) // 2, fields, source]
                dst = halo.at[(1 - dz) // 2, fields, 1 - dy, target]
            yield n, (dx, dy, dz), pltpu.make_async_remote_copy(
                src_ref=src, dst_ref=dst, send_sem=fine_send.at[n], recv_sem=fine_recv.at[n],
                device_id=device((dx, dy, dz)), device_id_type=MESH,
            )

    def deep_copies(part):
        fields = pl.ds(0, 2) if part == 0 else pl.ds(2, 1)
        for n, (dx, dy, dz) in enumerate(DEEP):
            yield n, (dx, dy, dz), pltpu.make_async_remote_copy(
                src_ref=coarse_own.at[fields],
                dst_ref=coarse_ext.at[fields, 1 - dy, 1 - dz, pl.ds(CX * gx, CX)],
                send_sem=deep_send.at[part, n], recv_sem=deep_recv.at[part, n],
                device_id=device((dx, dy, dz)), device_id_type=MESH,
            )

    def start(copies):
        for n, d, copy in copies:
            @pl.when(exists(d))
            def _(copy=copy):
                copy.start()

    def finish(copies):
        copies = list(copies)
        for n, d, copy in copies:
            @pl.when(exists(tuple(-s for s in d)))
            def _(copy=copy):
                copy.wait_recv()
        for n, d, copy in copies:
            @pl.when(exists(d))
            def _(copy=copy):
                copy.wait_send()

    def widen(field):
        ext[field, HX : HX + BX, 8:24] = own[field]
        lane, row = iota((LY, BZ), 1), iota((LY, BZ), 0)
        fits = (lane // 8) == (row + 8) % 16
        sides = []
        for side in (0, 1):
            rows = jnp.concatenate(
                [
                    jnp.broadcast_to(halo[side, field, 0], (LX, 8, BZ)),
                    jnp.broadcast_to(halo[side, field, 1], (LX, 16, BZ)),
                    jnp.broadcast_to(halo[side, field, 2], (LX, 8, BZ)),
                ],
                axis=1,
            )
            sides.append(jnp.where(fits[None], rows, 0.0).reshape(LX * LY, BZ))
        outer = select_dot(sides[0], m_unpack[:BZ]) + select_dot(sides[1], m_unpack[BZ:])
        wide[:, :, :BZ] = ext[field]
        wide[:, :, BZ:] = outer.reshape(LX, LY, BZ)

    def restrict_fine():
        t_fine[...] = select_dot(rest0[...].reshape(10 * LY, 2 * BZ), m_r0[...]).reshape(10, LY, BZ)
        return 0.5 * (t_fine[:, pl.ds(0, 16, stride=2)] + t_fine[:, pl.ds(1, 16, stride=2)])

    def restrict_mid(values):
        pairs = values.reshape(CX, 2, 16, BZ)
        pairs = pairs[:, 0] + pairs[:, 1]
        t_mid[...] = select_dot(pairs.reshape(CX * 16, BZ), m_r1[...]).reshape(CX, 16, BZ)
        cells = 0.5 * (t_mid[:, pl.ds(0, 8, stride=2)] + t_mid[:, pl.ds(1, 8, stride=2)])
        lane, row = iota((8, BZ), 1), iota((8, BZ), 0)
        return jnp.sum(jnp.where((lane // 32 == row - 2)[None], cells, 0.0), axis=1, keepdims=True)

    def put_coarse(field, cells):
        coarse_own[field] = cells
        coarse_ext[field, 1, 1, pl.ds(CX * gx, CX)] = cells

    def coarse_field(field):
        shape = (CX * nx, 16, BZ)
        lane, row = iota((16, BZ), 1), iota((16, BZ), 0)
        y = jnp.where(row < 10, row - 2, row - 18)
        slot, group = (y + 4) // 4, (row + 2) % 4
        total = None
        for dz in (-1, 0, 1):
            rows = jnp.zeros(shape, F32)
            for dy in (-1, 0, 1):
                fits = jnp.logical_and(slot == dy + 1, lane // 32 == group)
                taken = jnp.broadcast_to(coarse_ext[field, dy + 1, dz + 1], shape)
                rows = jnp.where(fits[None], taken, rows)
            rows = rows + pltpu.roll(rows, 32, 2)
            rows = rows + pltpu.roll(rows, 64, 2)
            rows = jnp.where((lane // 32 == dz % 4)[None], rows, 0.0)
            total = rows if total is None else total + rows
        return total

    def inside(layer, low, size, first, shape, x_first, y_of, z_of):
        pass

    def masked_inverse(values, x, y, z, scale):
        ok = jnp.logical_and(y >= 0, y < scale * CY * ny)
        ok = jnp.logical_and(ok, jnp.logical_and(z >= 0, z < scale * CZ * nz))
        if x is not None:
            ok = jnp.logical_and(ok, jnp.logical_and(x >= 0, x < scale * CX * nx))
        return jnp.where(ok, 0.6 / (26.0 + values), 0.0)

    def coefficients():
        lane, row = iota((LY, 2 * BZ), 1), iota((LY, 2 * BZ), 0)
        y, z = BY * gy + row - 8, BZ * gz + wrapped(lane, 256)

        def body(i):
            inv0[i] = masked_inverse(wide[i], BX * gx + i - HX, y, z, 4)

        loop(LX, 2, body)

        def pairs(j):
            rest0[j] = wide[2 * j + 1] + wide[2 * j + 2]

        loop(10, 2, pairs)
        c1 = restrict_fine()
        put_coarse(1, restrict_mid(c1[2:8]))
        shape = (10, 16, BZ)
        x = 2 * CX * gx + iota(shape, 0) - 2
        y = 2 * CY * gy + iota(shape, 1) - 4
        z = 2 * CZ * gz + wrapped(iota(shape, 2), 128)
        inv1[...] = masked_inverse(c1, x, y, z, 2)

    def down():
        def guess(i):
            e0[i] = inv0[i] * wide[i]

        loop(LX, 2, guess)

        def rest(j):
            i = 2 * j
            e_0, e_1, e_2, e_3 = e0[i], e0[i + 1], e0[i + 2], e0[i + 3]
            middle = e_1 + e_2
            total = around(e_0 + middle + (middle + e_3)) - middle
            rest0[j] = 0.4 * (wide[i + 1] + wide[i + 2]) + total

        loop(10, 2, rest)
        right = restrict_fine()
        g1[...] = right
        first = inv1[...] * right
        e1[...] = first
        total = first[1:7] + first[2:8] + first[3:9]
        remainder = 0.4 * right[2:8] + around(total) - first[2:8]
        return restrict_mid(remainder)

    def solve_coarsest(right):
        inverse = inv2[...]
        edge = jnp.zeros((1, 16, BZ), F32)
        e = inverse * right
        for _ in range(3):
            padded = jnp.concatenate([edge, e, edge], axis=0)
            total = around(padded[:-2] + padded[1:-1] + padded[2:])
            e = 0.4 * e + inverse * (right + total - e)
        coarse[pl.ds(1, CX * nx)] = e

    def up(keep):
        near = coarse[pl.ds(CX * gx, CX + 2)][:, :8]
        p_mid[:, pl.ds(0, 8, stride=2)] = near
        p_mid[:, pl.ds(1, 8, stride=2)] = near
        rise = select_dot(p_mid[...].reshape(5 * 16, BZ), m_p1[...]).reshape(5, 1, 16, BZ)
        rise = jnp.broadcast_to(rise, (5, 2, 16, BZ)).reshape(10, 16, BZ)
        e = e1[...] + rise
        total = around(e[0:8] + e[1:9] + e[2:10])
        e = 0.4 * e[1:9] + inv1[1:9] * (g1[1:9] + total - e[1:9])
        p_fine[:, pl.ds(0, 16, stride=2)] = e
        p_fine[:, pl.ds(1, 16, stride=2)] = e
        rest0[pl.ds(0, 8)] = select_dot(p_fine[...].reshape(8 * LY, BZ), m_p0[...]).reshape(8, LY, 2 * BZ)

        def add(j):
            i = 2 * j + 3
            e0[i] = e0[i] + rest0[j]
            e0[i + 1] = e0[i + 1] + rest0[j]

        loop(8, 2, add)

        def smooth(k):
            i = k + 4
            e = e0[i]
            total = around(e0[i - 1] + e + e0[i + 1])
            keep(i, 0.4 * e + inv0[i] * (wide[i] + total - e))

        loop(14, 2, smooth)

    def operate(keep):
        def body(x):
            i = x + HX
            value = wide[i]
            total = around(wide[i - 1] + value + wide[i + 1])
            value, total = value[8:24, :BZ], total[8:24, :BZ]
            keep(x, value, (27.0 + own[1, x]) * value - total)

        loop(BX, 2, body)

    def keep_wide(i, plane):
        wide[i] = plane

    for load in loads:
        load.wait()
    pack(0)
    pack(1)
    count = jnp.int32(0)
    for d in DEEP:
        count = count + exists(d).astype(jnp.int32)
    pl.semaphore_wait(barrier, count)

    start(fine_copies(0, 2))
    finish(fine_copies(0, 2))
    widen(1)
    coefficients()
    widen(0)
    put_coarse(0, down())
    start(deep_copies(0))
    finish(deep_copies(0))
    shape = (CX * nx, 16, BZ)
    row = iota(shape, 1)
    y = CY * gy + jnp.where(row < 10, row - 2, row - 18)
    z = CZ * gz + wrapped(iota(shape, 2), 128)
    inv2[...] = masked_inverse(coarse_field(1), None, y, z, 1)
    edge = jnp.zeros((16, BZ), F32)
    coarse[0] = edge
    coarse[CX * nx + 1] = edge
    solve_coarsest(coarse_field(0))
    up(keep_wide)

    sums_out[...] = jnp.zeros_like(sums_out)

    def first_image(x, value, image):
        p_out[x] = value
        image_out[x] = image
        own[2, x] = image
        sums_out[0] += own[0, x] * value
        sums_out[1] += image * value

    operate(first_image)

    pack(2)
    start(fine_copies(2, 1))
    finish(fine_copies(2, 1))
    widen(2)
    put_coarse(2, down())
    start(deep_copies(1))
    finish(deep_copies(1))
    solve_coarsest(coarse_field(2))
    up(keep_wide)

    def second_image(x, value, image):
        mw_out[x] = value
        nw_out[x] = image

    operate(second_image)


def call(sizes, right_side, coefficient):
    nx = sizes[0]
    block = jax.ShapeDtypeStruct((BX, BY, BZ), F32)
    any_spec = pl.BlockSpec(memory_space=pl.ANY)
    vmem_spec = pl.BlockSpec(memory_space=pltpu.VMEM)
    vmem = pltpu.VMEM
    return pl.pallas_call(
        functools.partial(kernel, sizes),
        out_shape=[block] * 4 + [jax.ShapeDtypeStruct((2, BY, BZ), F32)],
        in_specs=[any_spec] * 2,
        out_specs=[vmem_spec] * 5,
        scratch_shapes=[
            vmem((3, BX, BY, BZ), F32),
            vmem((3, LX, LY, BZ), F32),
            vmem((2, 3, BX, 1, BZ), F32),
            vmem((2, 3, 3, LX, 1, BZ), F32),
            vmem((3, CX, 1, BZ), F32),
            vmem((3, 3, 3, CX * nx, 1, BZ), F32),
            vmem((LX, LY, 2 * BZ), F32),
            vmem((LX, LY, 2 * BZ), F32),
            vmem((LX, LY, 2 * BZ), F32),
            vmem((10, LY, 2 * BZ), F32),
            vmem((10, 16, BZ), F32),
            vmem((10, 16, BZ), F32),
            vmem((10, 16, BZ), F32),
            vmem((CX * nx, 16, BZ), F32),
            vmem((CX * nx + 2, 16, BZ), F32),
            vmem((10, LY, BZ), F32),
            vmem((CX, 16, BZ), F32),
            vmem((5, 16, BZ), F32),
            vmem((8, LY, BZ), F32),
            vmem((BZ, 2 * BZ), BF16),
            vmem((2 * BZ, BZ), BF16),
            vmem((2 * BZ, BZ), BF16),
            vmem((BZ, BZ), BF16),
            vmem((BZ, BZ), BF16),
            vmem((BZ, 2 * BZ), BF16),
            pltpu.SemaphoreType.DMA((2,)),
            pltpu.SemaphoreType.DMA((len(FINE),)),
            pltpu.SemaphoreType.DMA((len(FINE),)),
            pltpu.SemaphoreType.DMA((2, len(DEEP))),
            pltpu.SemaphoreType.DMA((2, len(DEEP))),
        ],
        compiler_params=pltpu.CompilerParams(collective_id=0, has_side_effects=True),
    )(right_side, coefficient)


def solution(mesh):
    sizes = tuple(mesh.shape[axis] for axis in ("gx", "gy", "gz"))

    def shards(right_side, coefficient):
        precond, image, mw, nw, sums = call(sizes, right_side, coefficient)
        totals = lax.psum(jnp.sum(sums, axis=(1, 2)), ("gx", "gy", "gz"))
        alpha = totals[0] / totals[1]
        return (
            alpha * precond,
            right_side - alpha * image,
            precond - alpha * mw,
            image - alpha * nw,
        )

    spec = P("gx", "gy", "gz")
    return jax.shard_map(
        shards, mesh=mesh, in_specs=(spec, spec), out_specs=(spec,) * 4, check_vma=False
    )
```

time: 438 us -> 179 us (0.41)
  starting transfers between devices: 206 us -> 0 us
  waiting for transfers between devices: 119 us -> 0 us
  blocking collectives: 55.4 us -> 126 us
  Pallas kernels: 0 us -> 47.7 us
  local copies, waits for them, and re-layouts: 30 us -> 0.59 us
  other arithmetic: 21 us -> 2.61 us
    ppermute x72 -> x0, starting transfers between devices: 206 us -> none  [the longest x36 142 us: with_halo(): lax.ppermute(lax.slice_in_dim(block, block.shape[dim] - width, None, axis...]
    ppermute x72 -> x0, waiting for transfers between devices: 119 us -> none  [the longest x36 109 us: with_halo(): lax.ppermute(lax.slice_in_dim(block, 0, width, axis=dim), axis, backward)]
    psum x4 -> x1, blocking collectives: 55.4 us -> 126 us  [shards(): totals = lax.psum(jnp.sum(sums, axis=(1, 2)), ('gx', 'gy', 'gz'))]
    pallas_call x0 -> x1, Pallas kernels: none -> 47.7 us  [call(): pl.pallas_call(functools.partial(kernel, sizes), out_shape=[block] * 4 +...]
    reshape x13 -> x0, local copies, waits for them, and re-layouts: 26.3 us -> none  [the longest x5 25.2 us: restrict(): values.reshape(extent[0] // 2, 2, extent[1] // 2, 2, extent[2] // 2, 2)]
    reduce_sum x7 -> x1, other arithmetic: 10.9 us -> 0.82 us  [shards(): totals = lax.psum(jnp.sum(sums, axis=(1, 2)), ('gx', 'gy', 'gz'))]
  transfers between devices with their start and end apart: 72 -> 0, of which waited for: 40 -> 0; matrix products, arithmetic and copies ran while one was open for 3% -> 0% of each run, Pallas kernels for 0% -> 0%
where the time goes in v1:
time: 179 us
  blocking collectives  126 us (70%)
  Pallas kernels  47.7 us (27%)
  other arithmetic  2.61 us (1%)
  between operations  1.99 us (1%)
    psum x1, blocking collectives, shards(): totals = lax.psum(jnp.sum(sums, axis=(1, 2)), ('gx', 'gy', 'gz'))  126 us
    pallas_call x1, Pallas kernels, call(): pl.pallas_call(functools.partial(kernel, sizes), out_shape=[block] * 4 +...  47.7 us

profile of v1, /device:TPU:1, one launch (start us, length us, event | category | flops | bytes accessed | tf_op | source)
XLA Modules:
  0.0 178.6 jit_solution(9836567903750904173)
XLA Ops:
  0.6 0.0 copy-start
  0.6 47.7 %shard_map.57 = (f32[12,16,128]{2,1,0:T(8,128)}, f32[12,16,128]{2,1,0:T(8,128)}, f32[12,16,128]{2,1,0:T(8,128)}, f32[12,16,128]{2,1,0:T(8,128)}, f32[2,16,128]{2,1,0:T(8,128)}) custom-call(f32[12,16,128]{2,1,0:T(8,128)} %g_hbm.1, f32[12,16,128]{2,1,0:T(8,128)} %c_hbm.1), custom_call_target="tpu_custom_call" | custom-call | tf_op jit(solution)/shard_map/pallas_call | solution.py:401
  48.4 0.8 reduce_sum.9
  49.2 125.7 %psum.7 = f32[2]{0:T(128)S(1)} all-reduce(f32[2]{0:T(128)S(1)} %reduce_sum.9), channel_id=1, replica_groups=mesh['gx'=4,'gy'=16,'gz'=16] {'gx','gy','gz'}, use_global_device_ids=true, to_apply=%region_1.0 | all-reduce | flops 2 | bytes 16 | tf_op jit(solution)/shard_map/psum | solution.py:447
  174.9 0.6 fusion
  176.8 0.0 copy-done
  176.8 1.8 %multiply_subtract_fusion = (f32[12,16,128]{2,1,0:T(8,128)}, f32[12,16,128]{2,1,0:T(8,128)}, f32[12,16,128]{2,1,0:T(8,128)}, f32[12,16,128]{2,1,0:T(8,128)}) fusion(f32[12,16,128]{2,1,0:T(8,128)} %get-tuple-element.11, f32[12,16,128]{2,1,0:T(8,128)} %get-tuple-element.13, f32[]{:T(128)} %bitcast, f32[12,16,128]{2,1,0:T(8,128)S(1)} %copy-done, ...), kind=kLoop, calls=%fused_computation | loop fusion | flops 172032 | bytes 884740 | tf_op jit(solution)/shard_map/sub | solution.py:453
Async XLA Ops:
  0.6 176.2 %copy-start = (f32[12,16,128]{2,1,0:T(8,128)S(1)}, f32[12,16,128]{2,1,0:T(8,128)}, u32[]{:S(2)}) copy-start(f32[12,16,128]{2,1,0:T(8,128)} %g_hbm.1) | copy-start | bytes 294916

commit v2 on v1

--- a/solution.py
+++ b/solution.py
@@ -76,12 +76,13 @@
 def kernel(
     sizes,
     g_hbm, c_hbm,
-    p_out, image_out, mw_out, nw_out, sums_out,
+    p_out, image_out, mw_out, nw_out, alpha_out,
     own, ext, packed, halo, coarse_own, coarse_ext,
     wide, inv0, e0, rest0, inv1, g1, e1, inv2, coarse,
     t_fine, t_mid, p_mid, p_fine,
     m_pack, m_unpack, m_r0, m_r1, m_p1, m_p0,
-    load_sem, fine_send, fine_recv, deep_send, deep_recv,
+    sums, line_own, line_0, line_1, line_2,
+    load_sem, fine_send, fine_recv, deep_send, deep_recv, line_send, line_recv,
 ):
     nx, ny, nz = sizes
     gx, gy, gz = lax.axis_index("gx"), lax.axis_index("gy"), lax.axis_index("gz")
@@ -98,6 +99,11 @@
     def device(d):
         return (gx + d[0], gy + d[1], gz + d[2])
 
+    def along(axis, k):
+        at = [gx, gy, gz]
+        at[axis] = lax.rem(at[axis] + k, sizes[axis])
+        return tuple(at)
+
     loads = [
         pltpu.make_async_copy(g_hbm, own.at[0], load_sem.at[0]),
         pltpu.make_async_copy(c_hbm, own.at[1], load_sem.at[1]),
@@ -110,10 +116,19 @@
     coarse_ext[...] = jnp.zeros_like(coarse_ext)
 
     barrier = pltpu.get_barrier_semaphore()
+    count = jnp.int32(sum(sizes) - 3)
     for d in DEEP:
+        if sum(s != 0 for s in d) == 1:
+            continue
+        count = count + exists(d).astype(jnp.int32)
+
         @pl.when(exists(d))
         def _(d=d):
             pl.semaphore_signal(barrier, inc=1, device_id=device(d), device_id_type=MESH)
+
+    for axis in range(3):
+        for k in range(1, sizes[axis]):
+            pl.semaphore_signal(barrier, inc=1, device_id=along(axis, k), device_id_type=MESH)
 
     row, col = iota((BZ, 2 * BZ), 0), iota((BZ, 2 * BZ), 1)
     m_pack[...] = ones_where(row == jnp.where(col < BZ, col % 8, 120 + col % 8))
@@ -178,6 +193,31 @@
             @pl.when(exists(d))
             def _(copy=copy):
                 copy.wait_send()
+
+    lines = (line_0, line_1, line_2)
+
+    def line_copies(axis):
+        me = (gx, gy, gz)[axis]
+        for k in range(1, sizes[axis]):
+            yield pltpu.make_async_remote_copy(
+                src_ref=line_own.at[axis], dst_ref=lines[axis].at[me],
+                send_sem=line_send.at[axis, k], recv_sem=line_recv.at[axis, k],
+                device_id=along(axis, k), device_id_type=MESH,
+            )
+
+    def line_start(axis, row):
+        line_own[axis] = row
+        lines[axis][(gx, gy, gz)[axis]] = row
+        for copy in line_copies(axis):
+            copy.start()
+
+    def line_finish(axis):
+        copies = list(line_copies(axis))
+        for copy in copies:
+            copy.wait_recv()
+        for copy in copies:
+            copy.wait_send()
+        return jnp.sum(lines[axis][...], axis=0)
 
     def widen(field):
         ext[field, HX : HX + BX, 8:24] = own[field]
@@ -232,9 +272,6 @@
             total = rows if total is None else total + rows
         return total
 
-    def inside(layer, low, size, first, shape, x_first, y_of, z_of):
-        pass
-
     def masked_inverse(values, x, y, z, scale):
         ok = jnp.logical_and(y >= 0, y < scale * CY * ny)
         ok = jnp.logical_and(ok, jnp.logical_and(z >= 0, z < scale * CZ * nz))
@@ -340,9 +377,6 @@
         load.wait()
     pack(0)
     pack(1)
-    count = jnp.int32(0)
-    for d in DEEP:
-        count = count + exists(d).astype(jnp.int32)
     pl.semaphore_wait(barrier, count)
 
     start(fine_copies(0, 2))
@@ -364,32 +398,42 @@
     solve_coarsest(coarse_field(0))
     up(keep_wide)
 
-    sums_out[...] = jnp.zeros_like(sums_out)
+    sums[...] = jnp.zeros_like(sums)
 
     def first_image(x, value, image):
         p_out[x] = value
         image_out[x] = image
         own[2, x] = image
-        sums_out[0] += own[0, x] * value
-        sums_out[1] += image * value
+        sums[0] += own[0, x] * value
+        sums[1] += image * value
 
     operate(first_image)
-
     pack(2)
     start(fine_copies(2, 1))
+    gamma = jnp.sum(sums[0], axis=0, keepdims=True)
+    delta = jnp.sum(sums[1], axis=0, keepdims=True)
+    low = iota((1, BZ), 1) < 64
+    gamma, delta = gamma + pltpu.roll(gamma, 64, 1), delta + pltpu.roll(delta, 64, 1)
+    line_start(2, jnp.where(low, gamma, delta))
     finish(fine_copies(2, 1))
     widen(2)
     put_coarse(2, down())
     start(deep_copies(1))
+    line_start(1, line_finish(2))
     finish(deep_copies(1))
     solve_coarsest(coarse_field(2))
     up(keep_wide)
+    line_start(0, line_finish(1))
 
     def second_image(x, value, image):
         mw_out[x] = value
         nw_out[x] = image
 
     operate(second_image)
+    total = line_finish(0)
+    gamma = jnp.sum(jnp.where(low, total, 0.0), axis=1, keepdims=True)
+    delta = jnp.sum(jnp.where(low, 0.0, total), axis=1, keepdims=True)
+    alpha_out[...] = jnp.broadcast_to(gamma / delta, alpha_out.shape)
 
 
 def call(sizes, right_side, coefficient):
@@ -400,7 +444,7 @@
     vmem = pltpu.VMEM
     return pl.pallas_call(
         functools.partial(kernel, sizes),
-        out_shape=[block] * 4 + [jax.ShapeDtypeStruct((2, BY, BZ), F32)],
+        out_shape=[block] * 4 + [jax.ShapeDtypeStruct((1, BZ), F32)],
         in_specs=[any_spec] * 2,
         out_specs=[vmem_spec] * 5,
         scratch_shapes=[
@@ -429,11 +473,18 @@
             vmem((BZ, BZ), BF16),
             vmem((BZ, BZ), BF16),
             vmem((BZ, 2 * BZ), BF16),
+            vmem((2, BY, BZ), F32),
+            vmem((3, 1, BZ), F32),
+            vmem((sizes[0], 1, BZ), F32),
+            vmem((sizes[1], 1, BZ), F32),
+            vmem((sizes[2], 1, BZ), F32),
             pltpu.SemaphoreType.DMA((2,)),
             pltpu.SemaphoreType.DMA((len(FINE),)),
             pltpu.SemaphoreType.DMA((len(FINE),)),
             pltpu.SemaphoreType.DMA((2, len(DEEP))),
             pltpu.SemaphoreType.DMA((2, len(DEEP))),
+            pltpu.SemaphoreType.DMA((3, max(sizes))),
+            pltpu.SemaphoreType.DMA((3, max(sizes))),
         ],
         compiler_params=pltpu.CompilerParams(collective_id=0, has_side_effects=True),
     )(right_side, coefficient)
@@ -443,9 +494,8 @@
     sizes = tuple(mesh.shape[axis] for axis in ("gx", "gy", "gz"))
 
     def shards(right_side, coefficient):
-        precond, image, mw, nw, sums = call(sizes, right_side, coefficient)
-        totals = lax.psum(jnp.sum(sums, axis=(1, 2)), ("gx", "gy", "gz"))
-        alpha = totals[0] / totals[1]
+        precond, image, mw, nw, alpha = call(sizes, right_side, coefficient)
+        alpha = alpha[None]
         return (
             alpha * precond,
             right_side - alpha * image,

time: 179 us -> 64.9 us (0.36)
  blocking collectives: 126 us -> 0 us
  Pallas kernels: 47.7 us -> 61.7 us
    psum x1 -> x0, blocking collectives: 126 us -> none  [shards(): totals = lax.psum(jnp.sum(sums, axis=(1, 2)), ('gx', 'gy', 'gz'))]
    pallas_call x1, Pallas kernels: 47.7 us -> 61.7 us  [call(): pl.pallas_call(functools.partial(kernel, sizes), out_shape=[block] * 4 +...]
where the time goes in v2:
time: 64.9 us; the launch traced here: 64.8 us
  Pallas kernels  61.7 us (95%)
  other arithmetic  1.78 us (3%)
  between operations  0.66 us (1%)
  local copies, waits for them, and re-layouts  0.65 us (1%)
    pallas_call x1, Pallas kernels, call(): pl.pallas_call(functools.partial(kernel, sizes), out_shape=[block] * 4 +...  61.7 us
    sub x1, other arithmetic, shards(): image - alpha * nw  1.78 us

profile of v2, /device:TPU:1, one launch (start us, length us, event | category | flops | bytes accessed | tf_op | source)
XLA Modules:
  0.0 64.8 jit_solution(14687052213364477326)
XLA Ops:
  0.6 0.0 copy-start
  0.6 61.7 %shard_map.57 = (f32[12,16,128]{2,1,0:T(8,128)}, f32[12,16,128]{2,1,0:T(8,128)}, f32[12,16,128]{2,1,0:T(8,128)}, f32[12,16,128]{2,1,0:T(8,128)}, f32[1,128]{1,0:T(1,128)}) custom-call(f32[12,16,128]{2,1,0:T(8,128)} %g_hbm.1, f32[12,16,128]{2,1,0:T(8,128)} %c_hbm.1), custom_call_target="tpu_custom_call" | custom-call | tf_op jit(solution)/shard_map/pallas_call | solution.py:445
  62.3 0.0 copy-start.1
  62.3 0.0 copy-done
  62.3 0.6 copy-done.1
  63.0 1.8 %multiply_subtract_fusion = (f32[12,16,128]{2,1,0:T(8,128)}, f32[12,16,128]{2,1,0:T(8,128)}, f32[12,16,128]{2,1,0:T(8,128)}, f32[12,16,128]{2,1,0:T(8,128)}) fusion(f32[12,16,128]{2,1,0:T(8,128)} %get-tuple-element.11, f32[12,16,128]{2,1,0:T(8,128)} %get-tuple-element.13, f32[128]{0:T(128)S(1)} %bitcast.1, f32[12,16,128]{2,1,0:T(8,128)S(1)} %copy-done, ...), kind=kLoop, calls=%fused_computation | loop fusion | flops 172032 | bytes 885248 | tf_op jit(solution)/shard_map/sub | solution.py:503
Async XLA Ops:
  0.6 61.7 %copy-start = (f32[12,16,128]{2,1,0:T(8,128)S(1)}, f32[12,16,128]{2,1,0:T(8,128)}, u32[]{:S(2)}) copy-start(f32[12,16,128]{2,1,0:T(8,128)} %g_hbm.1) | copy-start | bytes 294916
  62.3 0.7 %copy-start.1 = (f32[1,128]{1,0:T(1,128)S(1)}, f32[1,128]{1,0:T(1,128)}, u32[]{:S(2)}) copy-start(f32[1,128]{1,0:T(1,128)} %get-tuple-element.9) | copy-start | bytes 1540

commit v3 on v2

--- a/solution.py
+++ b/solution.py
@@ -30,6 +30,8 @@
     for dz in (-1, 0, 1)
     if (dx, dy, dz) != (0, 0, 0)
 ]
+FINE.sort(key=lambda d: -sum(abs(s) for s in d))
+DEEP.sort(key=lambda d: -sum(abs(s) for s in d))
 
 
 def iota(shape, axis):
@@ -75,14 +77,14 @@
 
 def kernel(
     sizes,
-    g_hbm, c_hbm,
+    g_in, c_in,
     p_out, image_out, mw_out, nw_out, alpha_out,
     own, ext, packed, halo, coarse_own, coarse_ext,
     wide, inv0, e0, rest0, inv1, g1, e1, inv2, coarse,
     t_fine, t_mid, p_mid, p_fine,
     m_pack, m_unpack, m_r0, m_r1, m_p1, m_p0,
     sums, line_own, line_0, line_1, line_2,
-    load_sem, fine_send, fine_recv, deep_send, deep_recv, line_send, line_recv,
+    fine_send, fine_recv, deep_send, deep_recv, line_send, line_recv, hello,
 ):
     nx, ny, nz = sizes
     gx, gy, gz = lax.axis_index("gx"), lax.axis_index("gy"), lax.axis_index("gz")
@@ -104,20 +106,15 @@
         at[axis] = lax.rem(at[axis] + k, sizes[axis])
         return tuple(at)
 
-    loads = [
-        pltpu.make_async_copy(g_hbm, own.at[0], load_sem.at[0]),
-        pltpu.make_async_copy(c_hbm, own.at[1], load_sem.at[1]),
-    ]
-    for load in loads:
-        load.start()
-
     ext[...] = jnp.zeros_like(ext)
     halo[...] = jnp.zeros_like(halo)
     coarse_ext[...] = jnp.zeros_like(coarse_ext)
 
     barrier = pltpu.get_barrier_semaphore()
-    count = jnp.int32(sum(sizes) - 3)
-    for d in DEEP:
+    greeted = [(axis, k) for axis in range(2) for k in range(1, sizes[axis])]
+    greeted += [(2, k) for k in range(1, nz) if min(k, nz - k) <= 4]
+    count = jnp.int32(len(greeted))
+    for d in FINE:
         if sum(s != 0 for s in d) == 1:
             continue
         count = count + exists(d).astype(jnp.int32)
@@ -126,9 +123,8 @@
         def _(d=d):
             pl.semaphore_signal(barrier, inc=1, device_id=device(d), device_id_type=MESH)
 
-    for axis in range(3):
-        for k in range(1, sizes[axis]):
-            pl.semaphore_signal(barrier, inc=1, device_id=along(axis, k), device_id_type=MESH)
+    for axis, k in greeted:
+        pl.semaphore_signal(barrier, inc=1, device_id=along(axis, k), device_id_type=MESH)
 
     row, col = iota((BZ, 2 * BZ), 0), iota((BZ, 2 * BZ), 1)
     m_pack[...] = ones_where(row == jnp.where(col < BZ, col % 8, 120 + col % 8))
@@ -201,7 +197,7 @@
         for k in range(1, sizes[axis]):
             yield pltpu.make_async_remote_copy(
                 src_ref=line_own.at[axis], dst_ref=lines[axis].at[me],
-                send_sem=line_send.at[axis, k], recv_sem=line_recv.at[axis, k],
+                send_sem=line_send.at[axis], recv_sem=line_recv.at[axis],
                 device_id=along(axis, k), device_id_type=MESH,
             )
 
@@ -212,11 +208,13 @@
             copy.start()
 
     def line_finish(axis):
-        copies = list(line_copies(axis))
-        for copy in copies:
-            copy.wait_recv()
-        for copy in copies:
-            copy.wait_send()
+        rest = lines[axis].at[pl.ds(0, sizes[axis] - 1)]
+        whole = pltpu.make_async_remote_copy(
+            src_ref=rest, dst_ref=rest, send_sem=line_send.at[axis], recv_sem=line_recv.at[axis],
+            device_id=along(axis, 1), device_id_type=MESH,
+        )
+        whole.wait_recv()
+        whole.wait_send()
         return jnp.sum(lines[axis][...], axis=0)
 
     def widen(field):
@@ -373,13 +371,16 @@
     def keep_wide(i, plane):
         wide[i] = plane
 
-    for load in loads:
-        load.wait()
+    own[0] = g_in[...]
+    own[1] = c_in[...]
     pack(0)
     pack(1)
     pl.semaphore_wait(barrier, count)
 
     start(fine_copies(0, 2))
+    far = [k for k in (4, nz - 4) if nz > 8]
+    for k in far:
+        pl.semaphore_signal(hello, inc=1, device_id=along(2, k), device_id_type=MESH)
     finish(fine_copies(0, 2))
     widen(1)
     coefficients()
@@ -387,6 +388,8 @@
     put_coarse(0, down())
     start(deep_copies(0))
     finish(deep_copies(0))
+    if far:
+        pl.semaphore_wait(hello, len(far))
     shape = (CX * nx, 16, BZ)
     row = iota(shape, 1)
     y = CY * gy + jnp.where(row < 10, row - 2, row - 18)
@@ -414,23 +417,23 @@
     delta = jnp.sum(sums[1], axis=0, keepdims=True)
     low = iota((1, BZ), 1) < 64
     gamma, delta = gamma + pltpu.roll(gamma, 64, 1), delta + pltpu.roll(delta, 64, 1)
-    line_start(2, jnp.where(low, gamma, delta))
+    line_start(0, jnp.where(low, gamma, delta))
     finish(fine_copies(2, 1))
+    line_start(1, line_finish(0))
     widen(2)
     put_coarse(2, down())
     start(deep_copies(1))
-    line_start(1, line_finish(2))
+    line_start(2, line_finish(1))
     finish(deep_copies(1))
     solve_coarsest(coarse_field(2))
     up(keep_wide)
-    line_start(0, line_finish(1))
 
     def second_image(x, value, image):
         mw_out[x] = value
         nw_out[x] = image
 
     operate(second_image)
-    total = line_finish(0)
+    total = line_finish(2)
     gamma = jnp.sum(jnp.where(low, total, 0.0), axis=1, keepdims=True)
     delta = jnp.sum(jnp.where(low, 0.0, total), axis=1, keepdims=True)
     alpha_out[...] = jnp.broadcast_to(gamma / delta, alpha_out.shape)
@@ -439,13 +442,12 @@
 def call(sizes, right_side, coefficient):
     nx = sizes[0]
     block = jax.ShapeDtypeStruct((BX, BY, BZ), F32)
-    any_spec = pl.BlockSpec(memory_space=pl.ANY)
     vmem_spec = pl.BlockSpec(memory_space=pltpu.VMEM)
     vmem = pltpu.VMEM
     return pl.pallas_call(
         functools.partial(kernel, sizes),
         out_shape=[block] * 4 + [jax.ShapeDtypeStruct((1, BZ), F32)],
-        in_specs=[any_spec] * 2,
+        in_specs=[vmem_spec] * 2,
         out_specs=[vmem_spec] * 5,
         scratch_shapes=[
             vmem((3, BX, BY, BZ), F32),
@@ -478,15 +480,17 @@
             vmem((sizes[0], 1, BZ), F32),
             vmem((sizes[1], 1, BZ), F32),
             vmem((sizes[2], 1, BZ), F32),
-            pltpu.SemaphoreType.DMA((2,)),
             pltpu.SemaphoreType.DMA((len(FINE),)),
             pltpu.SemaphoreType.DMA((len(FINE),)),
             pltpu.SemaphoreType.DMA((2, len(DEEP))),
             pltpu.SemaphoreType.DMA((2, len(DEEP))),
-            pltpu.SemaphoreType.DMA((3, max(sizes))),
-            pltpu.SemaphoreType.DMA((3, max(sizes))),
+            pltpu.SemaphoreType.DMA((3,)),
+            pltpu.SemaphoreType.DMA((3,)),
+            pltpu.SemaphoreType.REGULAR,
         ],
-        compiler_params=pltpu.CompilerParams(collective_id=0, has_side_effects=True),
+        compiler_params=pltpu.CompilerParams(
+            collective_id=0, has_side_effects=True, vmem_limit_bytes=16 * 1024 * 1024
+        ),
     )(right_side, coefficient)
 
 

time: 64.9 us -> 60.5 us (0.932)
  Pallas kernels: 61.7 us -> 57.1 us
  local copies, waits for them, and re-layouts: 0.65 us -> 1.78 us
  other arithmetic: 1.78 us -> 0.75 us
    pallas_call x1, Pallas kernels: 61.7 us -> 57.1 us  [call(): pl.pallas_call(functools.partial(kernel, sizes), out_shape=[block] * 4 +...]
    unnamed x4, local copies, waits for them, and re-layouts: 0.65 us -> 1.78 us
    sub x1, other arithmetic: 1.78 us -> 0.75 us  [shards(): image - alpha * nw]
where the time goes in v3:
time: 60.5 us; the launch traced here: 60.3 us
  Pallas kernels  57.1 us (94%)
  local copies, waits for them, and re-layouts  1.78 us (3%)
  other arithmetic  0.75 us (1%)
  between operations  0.65 us (1%)
    pallas_call x1, Pallas kernels, call(): pl.pallas_call(functools.partial(kernel, sizes), out_shape=[block] * 4 +...  57.1 us
    unnamed x4, local copies, waits for them, and re-layouts  1.78 us

profile of v3, /device:TPU:1, one launch (start us, length us, event | category | flops | bytes accessed | tf_op | source)
XLA Modules:
  0.0 60.3 jit_solution(11006594421085680906)
XLA Ops:
  0.6 0.0 copy-start
  0.6 0.9 %copy-done = f32[12,16,128]{2,1,0:T(8,128)S(1)} copy-done((f32[12,16,128]{2,1,0:T(8,128)S(1)}, f32[12,16,128]{2,1,0:T(8,128)}, u32[]{:S(2)}) %copy-start) | copy-done | bytes 98328
  1.5 0.0 copy-start.1
  1.5 0.9 %copy-done.1 = f32[12,16,128]{2,1,0:T(8,128)S(1)} copy-done((f32[12,16,128]{2,1,0:T(8,128)S(1)}, f32[12,16,128]{2,1,0:T(8,128)}, u32[]{:S(2)}) %copy-start.1) | copy-done | bytes 98328
  2.4 57.1 %shard_map.57 = (f32[12,16,128]{2,1,0:T(8,128)S(1)}, f32[12,16,128]{2,1,0:T(8,128)S(1)}, f32[12,16,128]{2,1,0:T(8,128)S(1)}, f32[12,16,128]{2,1,0:T(8,128)S(1)}, f32[1,128]{1,0:T(1,128)S(1)}) custom-call(f32[12,16,128]{2,1,0:T(8,128)S(1)} %copy-done, f32[12,16,128]{2,1,0:T(8,128)S(1)} %copy-done.1), custom_call_target="tpu_custom_call" | custom-call | tf_op jit(solution)/shard_map/pallas_call | solution.py:447
  59.6 0.8 %multiply_subtract_fusion = (f32[12,16,128]{2,1,0:T(8,128)}, f32[12,16,128]{2,1,0:T(8,128)}, f32[12,16,128]{2,1,0:T(8,128)}, f32[12,16,128]{2,1,0:T(8,128)}) fusion(f32[12,16,128]{2,1,0:T(8,128)S(1)} %get-tuple-element.11, f32[12,16,128]{2,1,0:T(8,128)S(1)} %get-tuple-element.13, f32[128]{0:T(128)S(1)} %bitcast.1, f32[12,16,128]{2,1,0:T(8,128)S(1)} %copy-done, ...), kind=kLoop, calls=%fused_computation | loop fusion | flops 172032 | bytes 885248 | tf_op jit(solution)/shard_map/sub | solution.py:507
Async XLA Ops:
  0.6 0.9 %copy-start = (f32[12,16,128]{2,1,0:T(8,128)S(1)}, f32[12,16,128]{2,1,0:T(8,128)}, u32[]{:S(2)}) copy-start(f32[12,16,128]{2,1,0:T(8,128)} %g_in.1) | copy-start | bytes 294916
  1.5 0.9 %copy-start.1 = (f32[12,16,128]{2,1,0:T(8,128)S(1)}, f32[12,16,128]{2,1,0:T(8,128)}, u32[]{:S(2)}) copy-start(f32[12,16,128]{2,1,0:T(8,128)} %c_in.1) | copy-start | bytes 294916

commit v4 on v3

--- a/solution.py
+++ b/solution.py
@@ -79,12 +79,12 @@
     sizes,
     g_in, c_in,
     p_out, image_out, mw_out, nw_out, alpha_out,
-    own, ext, packed, halo, coarse_own, coarse_ext,
+    own, ext, packed, halo, coarse_own, coarse_ext, again_own, again_ext,
     wide, inv0, e0, rest0, inv1, g1, e1, inv2, coarse,
     t_fine, t_mid, p_mid, p_fine,
     m_pack, m_unpack, m_r0, m_r1, m_p1, m_p0,
     sums, line_own, line_0, line_1, line_2,
-    fine_send, fine_recv, deep_send, deep_recv, line_send, line_recv, hello,
+    load_sem, fine_send, fine_recv, deep_send, deep_recv, line_send, line_recv, hello,
 ):
     nx, ny, nz = sizes
     gx, gy, gz = lax.axis_index("gx"), lax.axis_index("gy"), lax.axis_index("gz")
@@ -106,9 +106,14 @@
         at[axis] = lax.rem(at[axis] + k, sizes[axis])
         return tuple(at)
 
+    loads = [pltpu.make_async_copy(r, own.at[n], load_sem.at[n]) for n, r in enumerate((g_in, c_in))]
+    for load in loads:
+        load.start()
+
     ext[...] = jnp.zeros_like(ext)
     halo[...] = jnp.zeros_like(halo)
     coarse_ext[...] = jnp.zeros_like(coarse_ext)
+    again_ext[...] = jnp.zeros_like(again_ext)
 
     barrier = pltpu.get_barrier_semaphore()
     greeted = [(axis, k) for axis in range(2) for k in range(1, sizes[axis])]
@@ -146,7 +151,8 @@
         packed[0, field] = flat[:, :, :BZ]
         packed[1, field] = flat[:, :, BZ:]
 
-    def fine_copies(first, count):
+    def fine_copies(part):
+        first, count = ((0, 2), (2, 1))[part]
         fields = pl.ds(first, count)
         for n, (dx, dy, dz) in enumerate(FINE):
             source = {-1: pl.ds(0, HX), 0: pl.ds(0, BX), 1: pl.ds(BX - HX, HX)}[dx]
@@ -159,16 +165,16 @@
                 src = packed.at[(dz + 1) // 2, fields, source]
                 dst = halo.at[(1 - dz) // 2, fields, 1 - dy, target]
             yield n, (dx, dy, dz), pltpu.make_async_remote_copy(
-                src_ref=src, dst_ref=dst, send_sem=fine_send.at[n], recv_sem=fine_recv.at[n],
+                src_ref=src, dst_ref=dst, send_sem=fine_send.at[part, n], recv_sem=fine_recv.at[part, n],
                 device_id=device((dx, dy, dz)), device_id_type=MESH,
             )
 
     def deep_copies(part):
-        fields = pl.ds(0, 2) if part == 0 else pl.ds(2, 1)
+        source, target = ((coarse_own, coarse_ext), (again_own, again_ext))[part]
         for n, (dx, dy, dz) in enumerate(DEEP):
             yield n, (dx, dy, dz), pltpu.make_async_remote_copy(
-                src_ref=coarse_own.at[fields],
-                dst_ref=coarse_ext.at[fields, 1 - dy, 1 - dz, pl.ds(CX * gx, CX)],
+                src_ref=source,
+                dst_ref=target.at[1 - dy, 1 - dz, pl.ds(CX * gx, CX)],
                 send_sem=deep_send.at[part, n], recv_sem=deep_recv.at[part, n],
                 device_id=device((dx, dy, dz)), device_id_type=MESH,
             )
@@ -180,11 +186,12 @@
                 copy.start()
 
     def finish(copies):
-        copies = list(copies)
         for n, d, copy in copies:
             @pl.when(exists(tuple(-s for s in d)))
             def _(copy=copy):
                 copy.wait_recv()
+
+    def sent(copies):
         for n, d, copy in copies:
             @pl.when(exists(d))
             def _(copy=copy):
@@ -207,14 +214,15 @@
         for copy in line_copies(axis):
             copy.start()
 
-    def line_finish(axis):
+    def line_whole(axis):
         rest = lines[axis].at[pl.ds(0, sizes[axis] - 1)]
-        whole = pltpu.make_async_remote_copy(
+        return pltpu.make_async_remote_copy(
             src_ref=rest, dst_ref=rest, send_sem=line_send.at[axis], recv_sem=line_recv.at[axis],
             device_id=along(axis, 1), device_id_type=MESH,
         )
-        whole.wait_recv()
-        whole.wait_send()
+
+    def line_finish(axis):
+        line_whole(axis).wait_recv()
         return jnp.sum(lines[axis][...], axis=0)
 
     def widen(field):
@@ -249,8 +257,12 @@
         return jnp.sum(jnp.where((lane // 32 == row - 2)[None], cells, 0.0), axis=1, keepdims=True)
 
     def put_coarse(field, cells):
-        coarse_own[field] = cells
-        coarse_ext[field, 1, 1, pl.ds(CX * gx, CX)] = cells
+        if field == 2:
+            again_own[...] = cells
+            again_ext[1, 1, pl.ds(CX * gx, CX)] = cells
+        else:
+            coarse_own[:, field] = cells
+            coarse_ext[1, 1, pl.ds(CX * gx, CX), field] = cells
 
     def coarse_field(field):
         shape = (CX * nx, 16, BZ)
@@ -262,7 +274,11 @@
             rows = jnp.zeros(shape, F32)
             for dy in (-1, 0, 1):
                 fits = jnp.logical_and(slot == dy + 1, lane // 32 == group)
-                taken = jnp.broadcast_to(coarse_ext[field, dy + 1, dz + 1], shape)
+                if field == 2:
+                    taken = again_ext[dy + 1, dz + 1]
+                else:
+                    taken = coarse_ext[dy + 1, dz + 1, :, field]
+                taken = jnp.broadcast_to(taken, shape)
                 rows = jnp.where(fits[None], taken, rows)
             rows = rows + pltpu.roll(rows, 32, 2)
             rows = rows + pltpu.roll(rows, 64, 2)
@@ -284,12 +300,12 @@
         def body(i):
             inv0[i] = masked_inverse(wide[i], BX * gx + i - HX, y, z, 4)
 
-        loop(LX, 2, body)
+        loop(LX, 22, body)
 
         def pairs(j):
             rest0[j] = wide[2 * j + 1] + wide[2 * j + 2]
 
-        loop(10, 2, pairs)
+        loop(10, 10, pairs)
         c1 = restrict_fine()
         put_coarse(1, restrict_mid(c1[2:8]))
         shape = (10, 16, BZ)
@@ -302,7 +318,7 @@
         def guess(i):
             e0[i] = inv0[i] * wide[i]
 
-        loop(LX, 2, guess)
+        loop(LX, 22, guess)
 
         def rest(j):
             i = 2 * j
@@ -311,7 +327,7 @@
             total = around(e_0 + middle + (middle + e_3)) - middle
             rest0[j] = 0.4 * (wide[i + 1] + wide[i + 2]) + total
 
-        loop(10, 2, rest)
+        loop(10, 10, rest)
         right = restrict_fine()
         g1[...] = right
         first = inv1[...] * right
@@ -348,7 +364,7 @@
             e0[i] = e0[i] + rest0[j]
             e0[i + 1] = e0[i + 1] + rest0[j]
 
-        loop(8, 2, add)
+        loop(8, 8, add)
 
         def smooth(k):
             i = k + 4
@@ -356,7 +372,7 @@
             total = around(e0[i - 1] + e + e0[i + 1])
             keep(i, 0.4 * e + inv0[i] * (wide[i] + total - e))
 
-        loop(14, 2, smooth)
+        loop(14, 14, smooth)
 
     def operate(keep):
         def body(x):
@@ -366,22 +382,22 @@
             value, total = value[8:24, :BZ], total[8:24, :BZ]
             keep(x, value, (27.0 + own[1, x]) * value - total)
 
-        loop(BX, 2, body)
+        loop(BX, 12, body)
 
     def keep_wide(i, plane):
         wide[i] = plane
 
-    own[0] = g_in[...]
-    own[1] = c_in[...]
+    for load in loads:
+        load.wait()
     pack(0)
     pack(1)
     pl.semaphore_wait(barrier, count)
 
-    start(fine_copies(0, 2))
+    start(fine_copies(0))
     far = [k for k in (4, nz - 4) if nz > 8]
     for k in far:
         pl.semaphore_signal(hello, inc=1, device_id=along(2, k), device_id_type=MESH)
-    finish(fine_copies(0, 2))
+    finish(fine_copies(0))
     widen(1)
     coefficients()
     widen(0)
@@ -412,13 +428,13 @@
 
     operate(first_image)
     pack(2)
-    start(fine_copies(2, 1))
+    start(fine_copies(1))
     gamma = jnp.sum(sums[0], axis=0, keepdims=True)
     delta = jnp.sum(sums[1], axis=0, keepdims=True)
     low = iota((1, BZ), 1) < 64
     gamma, delta = gamma + pltpu.roll(gamma, 64, 1), delta + pltpu.roll(delta, 64, 1)
     line_start(0, jnp.where(low, gamma, delta))
-    finish(fine_copies(2, 1))
+    finish(fine_copies(1))
     line_start(1, line_finish(0))
     widen(2)
     put_coarse(2, down())
@@ -433,6 +449,11 @@
         nw_out[x] = image
 
     operate(second_image)
+    for part in range(2):
+        sent(fine_copies(part))
+        sent(deep_copies(part))
+    for axis in range(3):
+        line_whole(axis).wait_send()
     total = line_finish(2)
     gamma = jnp.sum(jnp.where(low, total, 0.0), axis=1, keepdims=True)
     delta = jnp.sum(jnp.where(low, 0.0, total), axis=1, keepdims=True)
@@ -447,15 +468,17 @@
     return pl.pallas_call(
         functools.partial(kernel, sizes),
         out_shape=[block] * 4 + [jax.ShapeDtypeStruct((1, BZ), F32)],
-        in_specs=[vmem_spec] * 2,
+        in_specs=[pl.BlockSpec(memory_space=pltpu.HBM)] * 2,
         out_specs=[vmem_spec] * 5,
         scratch_shapes=[
             vmem((3, BX, BY, BZ), F32),
             vmem((3, LX, LY, BZ), F32),
             vmem((2, 3, BX, 1, BZ), F32),
             vmem((2, 3, 3, LX, 1, BZ), F32),
-            vmem((3, CX, 1, BZ), F32),
-            vmem((3, 3, 3, CX * nx, 1, BZ), F32),
+            vmem((CX, 2, 1, BZ), F32),
+            vmem((3, 3, CX * nx, 2, 1, BZ), F32),
+            vmem((CX, 1, BZ), F32),
+            vmem((3, 3, CX * nx, 1, BZ), F32),
             vmem((LX, LY, 2 * BZ), F32),
             vmem((LX, LY, 2 * BZ), F32),
             vmem((LX, LY, 2 * BZ), F32),
@@ -480,8 +503,9 @@
             vmem((sizes[0], 1, BZ), F32),
             vmem((sizes[1], 1, BZ), F32),
             vmem((sizes[2], 1, BZ), F32),
-            pltpu.SemaphoreType.DMA((len(FINE),)),
-            pltpu.SemaphoreType.DMA((len(FINE),)),
+            pltpu.SemaphoreType.DMA((2,)),
+            pltpu.SemaphoreType.DMA((2, len(FINE))),
+            pltpu.SemaphoreType.DMA((2, len(FINE))),
             pltpu.SemaphoreType.DMA((2, len(DEEP))),
             pltpu.SemaphoreType.DMA((2, len(DEEP))),
             pltpu.SemaphoreType.DMA((3,)),
@@ -498,7 +522,8 @@
     sizes = tuple(mesh.shape[axis] for axis in ("gx", "gy", "gz"))
 
     def shards(right_side, coefficient):
-        precond, image, mw, nw, alpha = call(sizes, right_side, coefficient)
+        held = [pltpu.with_memory_space_constraint(a, pltpu.HBM) for a in (right_side, coefficient)]
+        precond, image, mw, nw, alpha = call(sizes, *held)
         alpha = alpha[None]
         return (
             alpha * precond,

time: 60.5 us -> 56.9 us (0.940)
  Pallas kernels: 57.1 us -> 55.3 us
  local copies, waits for them, and re-layouts: 1.78 us -> 0.01 us
    pallas_call x1, Pallas kernels: 57.1 us -> 55.3 us  [call(): pl.pallas_call(functools.partial(kernel, sizes), out_shape=[block] * 4 +...]
    unnamed x4 -> x2, local copies, waits for them, and re-layouts: 1.78 us -> 0.01 us
where the time goes in v4:
time: 56.9 us; the launch traced here: 56.7 us
  Pallas kernels  55.3 us (97%)
  other arithmetic  0.76 us (1%)
  between operations  0.65 us (1%)
    pallas_call x1, Pallas kernels, call(): pl.pallas_call(functools.partial(kernel, sizes), out_shape=[block] * 4 +...  55.3 us

profile of v4, /device:TPU:1, one launch (start us, length us, event | category | flops | bytes accessed | tf_op | source)
XLA Modules:
  0.0 56.7 jit_solution(2689148763870924666)
XLA Ops:
  0.6 0.0 copy-start
  0.6 55.3 %shard_map.57 = (f32[12,16,128]{2,1,0:T(8,128)S(1)}, f32[12,16,128]{2,1,0:T(8,128)S(1)}, f32[12,16,128]{2,1,0:T(8,128)S(1)}, f32[12,16,128]{2,1,0:T(8,128)S(1)}, f32[1,128]{1,0:T(1,128)S(1)}) custom-call(f32[12,16,128]{2,1,0:T(8,128)} %g_in.1, f32[12,16,128]{2,1,0:T(8,128)} %c_in.1), custom_call_target="tpu_custom_call" | custom-call | tf_op jit(solution)/shard_map/pallas_call | solution.py:468
  56.0 0.0 copy-done
  56.0 0.8 %multiply_subtract_fusion = (f32[12,16,128]{2,1,0:T(8,128)}, f32[12,16,128]{2,1,0:T(8,128)}, f32[12,16,128]{2,1,0:T(8,128)}, f32[12,16,128]{2,1,0:T(8,128)}) fusion(f32[12,16,128]{2,1,0:T(8,128)S(1)} %get-tuple-element.11, f32[12,16,128]{2,1,0:T(8,128)S(1)} %get-tuple-element.13, f32[128]{0:T(128)S(1)} %bitcast.1, f32[12,16,128]{2,1,0:T(8,128)S(1)} %copy-done, ...), kind=kLoop, calls=%fused_computation | loop fusion | flops 172032 | bytes 885248 | tf_op jit(solution)/shard_map/sub | solution.py:532
Async XLA Ops:
  0.6 55.3 %copy-start = (f32[12,16,128]{2,1,0:T(8,128)S(1)}, f32[12,16,128]{2,1,0:T(8,128)}, u32[]{:S(2)}) copy-start(f32[12,16,128]{2,1,0:T(8,128)} %g_in.1) | copy-start | bytes 294916

commit v5 on v4

--- a/solution.py
+++ b/solution.py
@@ -83,7 +83,7 @@
     wide, inv0, e0, rest0, inv1, g1, e1, inv2, coarse,
     t_fine, t_mid, p_mid, p_fine,
     m_pack, m_unpack, m_r0, m_r1, m_p1, m_p0,
-    sums, line_own, line_0, line_1, line_2,
+    sums, line_own, line_0, line_1,
     load_sem, fine_send, fine_recv, deep_send, deep_recv, line_send, line_recv, hello,
 ):
     nx, ny, nz = sizes
@@ -100,6 +100,9 @@
 
     def device(d):
         return (gx + d[0], gy + d[1], gz + d[2])
+
+    def across(i, j):
+        return (lax.rem(gx + i, nx), lax.rem(gy + j, ny), gz)
 
     def along(axis, k):
         at = [gx, gy, gz]
@@ -197,33 +200,32 @@
             def _(copy=copy):
                 copy.wait_send()
 
-    lines = (line_0, line_1, line_2)
-
-    def line_copies(axis):
-        me = (gx, gy, gz)[axis]
-        for k in range(1, sizes[axis]):
-            yield pltpu.make_async_remote_copy(
-                src_ref=line_own.at[axis], dst_ref=lines[axis].at[me],
-                send_sem=line_send.at[axis], recv_sem=line_recv.at[axis],
-                device_id=along(axis, k), device_id_type=MESH,
-            )
-
-    def line_start(axis, row):
-        line_own[axis] = row
-        lines[axis][(gx, gy, gz)[axis]] = row
-        for copy in line_copies(axis):
-            copy.start()
-
-    def line_whole(axis):
-        rest = lines[axis].at[pl.ds(0, sizes[axis] - 1)]
+    planes = [(i, j) for i in range(nx) for j in range(ny) if (i, j) != (0, 0)]
+    phases = (line_0, line_1)
+    places = (gx * ny + gy, gz)
+    targets = ([across(i, j) for i, j in planes], [along(2, k) for k in range(1, nz)])
+
+    def line_copy(phase, source, target, device_id):
         return pltpu.make_async_remote_copy(
-            src_ref=rest, dst_ref=rest, send_sem=line_send.at[axis], recv_sem=line_recv.at[axis],
-            device_id=along(axis, 1), device_id_type=MESH,
+            src_ref=source, dst_ref=target,
+            send_sem=line_send.at[phase], recv_sem=line_recv.at[phase],
+            device_id=device_id, device_id_type=MESH,
         )
 
-    def line_finish(axis):
-        line_whole(axis).wait_recv()
-        return jnp.sum(lines[axis][...], axis=0)
+    def line_start(phase, row):
+        line_own[phase] = row
+        target = phases[phase].at[places[phase]]
+        phases[phase][places[phase]] = row
+        for device_id in targets[phase]:
+            line_copy(phase, line_own.at[phase], target, device_id).start()
+
+    def line_whole(phase):
+        rest = phases[phase].at[pl.ds(0, len(targets[phase]))]
+        return line_copy(phase, rest, rest, targets[phase][0])
+
+    def line_finish(phase):
+        line_whole(phase).wait_recv()
+        return jnp.sum(phases[phase][...], axis=0)
 
     def widen(field):
         ext[field, HX : HX + BX, 8:24] = own[field]
@@ -394,9 +396,9 @@
     pl.semaphore_wait(barrier, count)
 
     start(fine_copies(0))
-    far = [k for k in (4, nz - 4) if nz > 8]
-    for k in far:
-        pl.semaphore_signal(hello, inc=1, device_id=along(2, k), device_id_type=MESH)
+    far = [(2, k) for k in (4, nz - 4) if nz > 8] + [(0, k) for k in range(1, nx)]
+    for axis, k in far:
+        pl.semaphore_signal(hello, inc=1, device_id=along(axis, k), device_id_type=MESH)
     finish(fine_copies(0))
     widen(1)
     coefficients()
@@ -427,19 +429,19 @@
         sums[1] += image * value
 
     operate(first_image)
-    pack(2)
-    start(fine_copies(1))
     gamma = jnp.sum(sums[0], axis=0, keepdims=True)
     delta = jnp.sum(sums[1], axis=0, keepdims=True)
     low = iota((1, BZ), 1) < 64
     gamma, delta = gamma + pltpu.roll(gamma, 64, 1), delta + pltpu.roll(delta, 64, 1)
     line_start(0, jnp.where(low, gamma, delta))
+    start(copy for copy in fine_copies(1) if copy[1][2] == 0)
+    pack(2)
+    start(copy for copy in fine_copies(1) if copy[1][2] != 0)
     finish(fine_copies(1))
-    line_start(1, line_finish(0))
     widen(2)
     put_coarse(2, down())
     start(deep_copies(1))
-    line_start(2, line_finish(1))
+    line_start(1, line_finish(0))
     finish(deep_copies(1))
     solve_coarsest(coarse_field(2))
     up(keep_wide)
@@ -452,9 +454,9 @@
     for part in range(2):
         sent(fine_copies(part))
         sent(deep_copies(part))
-    for axis in range(3):
-        line_whole(axis).wait_send()
-    total = line_finish(2)
+    for phase in range(2):
+        line_whole(phase).wait_send()
+    total = line_finish(1)
     gamma = jnp.sum(jnp.where(low, total, 0.0), axis=1, keepdims=True)
     delta = jnp.sum(jnp.where(low, 0.0, total), axis=1, keepdims=True)
     alpha_out[...] = jnp.broadcast_to(gamma / delta, alpha_out.shape)
@@ -499,17 +501,16 @@
             vmem((BZ, BZ), BF16),
             vmem((BZ, 2 * BZ), BF16),
             vmem((2, BY, BZ), F32),
-            vmem((3, 1, BZ), F32),
-            vmem((sizes[0], 1, BZ), F32),
-            vmem((sizes[1], 1, BZ), F32),
+            vmem((2, 1, BZ), F32),
+            vmem((nx * sizes[1], 1, BZ), F32),
             vmem((sizes[2], 1, BZ), F32),
             pltpu.SemaphoreType.DMA((2,)),
             pltpu.SemaphoreType.DMA((2, len(FINE))),
             pltpu.SemaphoreType.DMA((2, len(FINE))),
             pltpu.SemaphoreType.DMA((2, len(DEEP))),
             pltpu.SemaphoreType.DMA((2, len(DEEP))),
-            pltpu.SemaphoreType.DMA((3,)),
-            pltpu.SemaphoreType.DMA((3,)),
+            pltpu.SemaphoreType.DMA((2,)),
+            pltpu.SemaphoreType.DMA((2,)),
             pltpu.SemaphoreType.REGULAR,
         ],
         compiler_params=pltpu.CompilerParams(

time: 56.9 us -> 53.7 us (0.944)
  Pallas kernels: 55.3 us -> 52.1 us
    pallas_call x1, Pallas kernels: 55.3 us -> 52.1 us  [call(): pl.pallas_call(functools.partial(kernel, sizes), out_shape=[block] * 4 +...]
where the time goes in v5:
time: 53.7 us; the launch traced here: 53.5 us
  Pallas kernels  52.1 us (97%)
  other arithmetic  0.76 us (1%)
  between operations  0.65 us (1%)
    pallas_call x1, Pallas kernels, call(): pl.pallas_call(functools.partial(kernel, sizes), out_shape=[block] * 4 +...  52.1 us

profile of v5, /device:TPU:1, one launch (start us, length us, event | category | flops | bytes accessed | tf_op | source)
XLA Modules:
  0.0 53.5 jit_solution(2110156880912799789)
XLA Ops:
  0.6 0.0 copy-start
  0.6 52.1 %shard_map.57 = (f32[12,16,128]{2,1,0:T(8,128)S(1)}, f32[12,16,128]{2,1,0:T(8,128)S(1)}, f32[12,16,128]{2,1,0:T(8,128)S(1)}, f32[12,16,128]{2,1,0:T(8,128)S(1)}, f32[1,128]{1,0:T(1,128)S(1)}) custom-call(f32[12,16,128]{2,1,0:T(8,128)} %g_in.1, f32[12,16,128]{2,1,0:T(8,128)} %c_in.1), custom_call_target="tpu_custom_call" | custom-call | tf_op jit(solution)/shard_map/pallas_call | solution.py:470
  52.7 0.0 copy-done
  52.7 0.8 %multiply_subtract_fusion = (f32[12,16,128]{2,1,0:T(8,128)}, f32[12,16,128]{2,1,0:T(8,128)}, f32[12,16,128]{2,1,0:T(8,128)}, f32[12,16,128]{2,1,0:T(8,128)}) fusion(f32[12,16,128]{2,1,0:T(8,128)S(1)} %get-tuple-element.11, f32[12,16,128]{2,1,0:T(8,128)S(1)} %get-tuple-element.13, f32[128]{0:T(128)S(1)} %bitcast.1, f32[12,16,128]{2,1,0:T(8,128)S(1)} %copy-done, ...), kind=kLoop, calls=%fused_computation | loop fusion | flops 172032 | bytes 885248 | tf_op jit(solution)/shard_map/sub | solution.py:533
Async XLA Ops:
  0.6 52.1 %copy-start = (f32[12,16,128]{2,1,0:T(8,128)S(1)}, f32[12,16,128]{2,1,0:T(8,128)}, u32[]{:S(2)}) copy-start(f32[12,16,128]{2,1,0:T(8,128)} %g_in.1) | copy-start | bytes 294916

commit v6 on v5

--- a/solution.py
+++ b/solution.py
@@ -154,21 +154,19 @@
         packed[0, field] = flat[:, :, :BZ]
         packed[1, field] = flat[:, :, BZ:]
 
-    def fine_copies(part):
-        first, count = ((0, 2), (2, 1))[part]
-        fields = pl.ds(first, count)
+    def fine_copies(field):
         for n, (dx, dy, dz) in enumerate(FINE):
             source = {-1: pl.ds(0, HX), 0: pl.ds(0, BX), 1: pl.ds(BX - HX, HX)}[dx]
             target = {-1: pl.ds(HX + BX, HX), 0: pl.ds(HX, BX), 1: pl.ds(0, HX)}[dx]
             if dz == 0:
                 rows = {-1: pl.ds(0, 8), 0: pl.ds(0, 16), 1: pl.ds(8, 8)}[dy]
                 to = {-1: pl.ds(24, 8), 0: pl.ds(8, 16), 1: pl.ds(0, 8)}[dy]
-                src, dst = own.at[fields, source, rows], ext.at[fields, target, to]
+                src, dst = own.at[field, source, rows], ext.at[field, target, to]
             else:
-                src = packed.at[(dz + 1) // 2, fields, source]
-                dst = halo.at[(1 - dz) // 2, fields, 1 - dy, target]
+                src = packed.at[(dz + 1) // 2, field, source]
+                dst = halo.at[(1 - dz) // 2, field, 1 - dy, target]
             yield n, (dx, dy, dz), pltpu.make_async_remote_copy(
-                src_ref=src, dst_ref=dst, send_sem=fine_send.at[part, n], recv_sem=fine_recv.at[part, n],
+                src_ref=src, dst_ref=dst, send_sem=fine_send.at[field, n], recv_sem=fine_recv.at[field, n],
                 device_id=device((dx, dy, dz)), device_id_type=MESH,
             )
 
@@ -395,13 +393,15 @@
     pack(1)
     pl.semaphore_wait(barrier, count)
 
+    start(fine_copies(1))
     start(fine_copies(0))
     far = [(2, k) for k in (4, nz - 4) if nz > 8] + [(0, k) for k in range(1, nx)]
     for axis, k in far:
         pl.semaphore_signal(hello, inc=1, device_id=along(axis, k), device_id_type=MESH)
-    finish(fine_copies(0))
+    finish(fine_copies(1))
     widen(1)
     coefficients()
+    finish(fine_copies(0))
     widen(0)
     put_coarse(0, down())
     start(deep_copies(0))
@@ -434,10 +434,10 @@
     low = iota((1, BZ), 1) < 64
     gamma, delta = gamma + pltpu.roll(gamma, 64, 1), delta + pltpu.roll(delta, 64, 1)
     line_start(0, jnp.where(low, gamma, delta))
-    start(copy for copy in fine_copies(1) if copy[1][2] == 0)
+    start(copy for copy in fine_copies(2) if copy[1][2] == 0)
     pack(2)
-    start(copy for copy in fine_copies(1) if copy[1][2] != 0)
-    finish(fine_copies(1))
+    start(copy for copy in fine_copies(2) if copy[1][2] != 0)
+    finish(fine_copies(2))
     widen(2)
     put_coarse(2, down())
     start(deep_copies(1))
@@ -451,8 +451,9 @@
         nw_out[x] = image
 
     operate(second_image)
+    for field in range(3):
+        sent(fine_copies(field))
     for part in range(2):
-        sent(fine_copies(part))
         sent(deep_copies(part))
     for phase in range(2):
         line_whole(phase).wait_send()
@@ -505,8 +506,8 @@
             vmem((nx * sizes[1], 1, BZ), F32),
             vmem((sizes[2], 1, BZ), F32),
             pltpu.SemaphoreType.DMA((2,)),
-            pltpu.SemaphoreType.DMA((2, len(FINE))),
-            pltpu.SemaphoreType.DMA((2, len(FINE))),
+            pltpu.SemaphoreType.DMA((3, len(FINE))),
+            pltpu.SemaphoreType.DMA((3, len(FINE))),
             pltpu.SemaphoreType.DMA((2, len(DEEP))),
             pltpu.SemaphoreType.DMA((2, len(DEEP))),
             pltpu.SemaphoreType.DMA((2,)),

time: 53.7 us -> 53.6 us (level)
  no operation moved by 1% of the time
where the time goes in v6:
time: 53.6 us; the launch traced here: 53.4 us
  Pallas kernels  52 us (97%)
  other arithmetic  0.76 us (1%)
  between operations  0.65 us (1%)
    pallas_call x1, Pallas kernels, call(): pl.pallas_call(functools.partial(kernel, sizes), out_shape=[block] * 4 +...  52 us

profile of v6, /device:TPU:1, one launch (start us, length us, event | category | flops | bytes accessed | tf_op | source)
XLA Modules:
  0.0 53.4 jit_solution(2394464500661901470)
XLA Ops:
  0.6 0.0 copy-start
  0.6 52.0 %shard_map.57 = (f32[12,16,128]{2,1,0:T(8,128)S(1)}, f32[12,16,128]{2,1,0:T(8,128)S(1)}, f32[12,16,128]{2,1,0:T(8,128)S(1)}, f32[12,16,128]{2,1,0:T(8,128)S(1)}, f32[1,128]{1,0:T(1,128)S(1)}) custom-call(f32[12,16,128]{2,1,0:T(8,128)} %g_in.1, f32[12,16,128]{2,1,0:T(8,128)} %c_in.1), custom_call_target="tpu_custom_call" | custom-call | tf_op jit(solution)/shard_map/pallas_call | solution.py:471
  52.6 0.0 copy-done
  52.6 0.8 %multiply_subtract_fusion = (f32[12,16,128]{2,1,0:T(8,128)}, f32[12,16,128]{2,1,0:T(8,128)}, f32[12,16,128]{2,1,0:T(8,128)}, f32[12,16,128]{2,1,0:T(8,128)}) fusion(f32[12,16,128]{2,1,0:T(8,128)S(1)} %get-tuple-element.11, f32[12,16,128]{2,1,0:T(8,128)S(1)} %get-tuple-element.13, f32[128]{0:T(128)S(1)} %bitcast.1, f32[12,16,128]{2,1,0:T(8,128)S(1)} %copy-done, ...), kind=kLoop, calls=%fused_computation | loop fusion | flops 172032 | bytes 885248 | tf_op jit(solution)/shard_map/sub | solution.py:534
Async XLA Ops:
  0.6 52.0 %copy-start = (f32[12,16,128]{2,1,0:T(8,128)S(1)}, f32[12,16,128]{2,1,0:T(8,128)}, u32[]{:S(2)}) copy-start(f32[12,16,128]{2,1,0:T(8,128)} %g_in.1) | copy-start | bytes 294916
